TPU v7x, 256 devices: a whole 4x4x8 slice. The times are simulated.
256 devices in a mesh: replica: 64 (over z, x, core), model: 4 (over y).
Axes of the slice: x: 4, y: 4, z: 8, core: 2. Of those that a mesh axis runs over, the one named last changes fastest.
Arguments:
- partial_query: float32 [64, 1280, 1280], P('replica', None, 'model'), may hold values from -1.75 to 1.75
- partial_key: float32 [64, 1280, 1280], P('replica', None, 'model'), may hold values from -1.75 to 1.75
- partial_value: float32 [64, 1280, 1280], P('replica', None, 'model'), may hold values from -1.75 to 1.75
- partial_mixed: float32 [64, 1280, 1280], P('replica', 'model'), may hold values from -1.75 to 1.75
- partial_norm: float32 [64, 1280], P('replica'), may hold values from -16 to 16
- master_query: float32 [1280, 1280], P('replica', 'model'), may hold values from -0.15625 to 0.15625
- master_key: float32 [1280, 1280], P('replica', 'model'), may hold values from -0.15625 to 0.15625
- master_value: float32 [1280, 1280], P('replica', 'model'), may hold values from -0.15625 to 0.15625
- master_mixed: float32 [1280, 1280], P('model', 'replica'), may hold values from -0.15625 to 0.15625
- master_norm: float32 [1280], P('replica'), may hold values from 0.25 to 1.75
Outputs:
- compute_query: bfloat16 [1280, 1280], P(None, 'model')
- compute_key: bfloat16 [1280, 1280], P(None, 'model')
- compute_value: bfloat16 [1280, 1280], P(None, 'model')
- compute_mixed: bfloat16 [1280, 1280], P('model')
- compute_norm: bfloat16 [1280], replicated
- stepped_query: float32 [1280, 1280], P('replica', 'model')
- stepped_key: float32 [1280, 1280], P('replica', 'model')
- stepped_value: float32 [1280, 1280], P('replica', 'model')
- stepped_mixed: float32 [1280, 1280], P('model', 'replica')
- stepped_norm: float32 [1280], P('replica')
All inputs are finite; a program needn't handle non-finite values.
Results may differ from a plain program's by a relative error of at most 0.001.
Values may be sent and summed in bfloat16 or wider, within the bound.
No kernel may reach another device: no remote copies, remote signals or barrier semaphores. Data moves between devices by JAX's collectives and lax.ppermute only.
A program may use at most 128 MiB of HBM per device.

v0:
```python
from functools import partial

import jax
import jax.numpy as jnp
from jax import lax
from jax.experimental import pallas as pl
from jax.experimental.pallas import tpu as pltpu
from jax.sharding import Mesh
from jax.sharding import PartitionSpec as P


learn_rate = 0.3
NZ, NX, NC = 8, 4, 2
CHIPS = ("z", "x", "c")
f32, bf16 = jnp.float32, jnp.bfloat16
ROWS, LANES, COLS, EXTRA = 40, 128, 5, 16
B_PIECES = ((0, 0, ROWS, 0), (1, 0, EXTRA, ROWS))
A_PIECES = ((2, 0, ROWS, 0), (3, 0, ROWS, ROWS), (4, 0, ROWS, 2 * ROWS), (1, EXTRA, ROWS, 3 * ROWS))
A_ROWS = 4 * ROWS - EXTRA
B_ROWS = ROWS + EXTRA + 8
G_ROWS = COLS * ROWS + 8
CHUNK = 32
SPLIT = 2 * LANES


def shift(v, dz, dx, dc=0):
    pairs = []
    for z in range(NZ):
        for x in range(NX):
            for c in range(NC):
                there = ((z + dz) % NZ * NX + (x + dx) % NX) * NC + (c ^ dc)
                pairs.append(((z * NX + x) * NC + c, there))
    return lax.ppermute(v, CHIPS, pairs)


def shift_x(v):
    far_one = shift(v[2], 0, 2)
    return [v[0], shift(v[1], 0, 1), far_one, shift(v[3], 0, 3)]


def spread(v):
    return lax.all_to_all(v, "z", 0, 0, tiled=True)


def block_copies(blocks, out, sems, lanes=pl.ds(0, 1280)):
    copies, at = [], 0
    for source, low, count in blocks:
        for r in range(0, count, CHUNK):
            rows, place = pl.ds(low + r, CHUNK), pl.ds(at, CHUNK)
            copies.append(pltpu.make_async_copy(source.at[rows, lanes], out.at[place, lanes], sems.at[at // CHUNK]))
            at += CHUNK
    return copies


def start_for(wanted, pairs, copies_of):
    for core in range(NC):

        @pl.when(lax.axis_index("c") == core)
        def _(core=core):
            for c in copies_of(pairs[wanted(core)]):
                c.start()


def blocks_b(q, v):
    return [[(q, 0, SPLIT)], [(v, 0, SPLIT)]]


def blocks_a(q, k, v, m):
    rest = 320 - SPLIT
    return [[(q, SPLIT, rest), (k, 0, 320)], [(v, SPLIT, rest), (m, 0, 320)]]


def pick_kernel(*refs):
    *sources, send, sems = refs
    pairs = (blocks_b if len(sources) == 2 else blocks_a)(*sources)
    copies_of = lambda blocks: block_copies(blocks, send, sems)
    start_for(lambda core: 1 - core, pairs, copies_of)
    for c in copies_of(pairs[0]):
        c.wait()


HALVES = (pl.ds(0, 640), pl.ds(640, 640))


def split_b_kernel(q, v, got, norm, *refs):
    *outs, extra, own, b, sems, out_sems = refs
    z0 = lax.axis_index("z")
    pairs = blocks_b(q, v)
    halves = lambda blocks: [block_copies(blocks, own, sems.at[i], HALVES[i]) for i in range(2)]
    start_for(lambda core: core, pairs, lambda blocks: sum(halves(blocks), []))
    steps = [lax.rem(z + NZ - z0, NZ) for z in range(NZ)]
    for z, step in enumerate(steps):
        b[step, :, B_ROWS - 8 :, :] = norm[z]
    for i, copies in enumerate(halves(pairs[0])):
        lanes, some = slice(640 * i, 640 * i + 640), slice(4 * i, 4 * i + 4)
        for t in range(2):
            rows = slice(LANES * t, LANES * t + LANES)
            for c in copies[LANES // CHUNK * t : LANES // CHUNK * (t + 1)]:
                c.wait()
            tile = (own[rows, lanes] + got[rows, lanes]).T.reshape(4, NX, ROWS, LANES)
            for z in range(4):
                if t == 0:
                    b[steps[4 * i + z], :, :ROWS, :] = tile[z]
                else:
                    b[steps[4 * i + z], :, ROWS : ROWS + EXTRA, :] = tile[z, :, :EXTRA]
            if t == 1:
                extra[some] = tile[:, :, EXTRA:]
    out_copies = [pltpu.make_async_copy(b.at[r], outs[r], out_sems.at[r]) for r in range(NZ)]
    for c in out_copies:
        c.start()
    for c in out_copies:
        c.wait()


def split_a_kernel(q, k, v, m, got, extra, a0, a1, a2, a3, own, turned, sems):
    x = lax.axis_index("x")
    pairs = blocks_a(q, k, v, m)
    halves = lambda blocks: [block_copies(blocks, own, sems.at[i], HALVES[i]) for i in range(2)]
    start_for(lambda core: core, pairs, lambda blocks: sum(halves(blocks), []))
    for j, a in enumerate((a0, a1, a2, a3)):
        a[:, 3 * ROWS :, :] = extra[:, lax.rem(x + j, NX)]
    for i, copies in enumerate(halves(pairs[0])):
        lanes = slice(640 * i, 640 * i + 640)
        for t in range(3):
            rows = slice(LANES * t, LANES * t + LANES)
            for c in copies[LANES // CHUNK * t : LANES // CHUNK * (t + 1)]:
                c.wait()
            turned[...] = (own[rows, lanes] + got[rows, lanes]).T.reshape(4, NX, ROWS, LANES)
            for j, a in enumerate((a0, a1, a2, a3)):
                a[4 * i : 4 * i + 4, ROWS * t : ROWS * t + ROWS, :] = turned[:, lax.rem(x + j, NX)]


def vmem(n):
    return [pl.BlockSpec(memory_space=pltpu.VMEM)] * n


def hbm(n):
    return [pl.BlockSpec(memory_space=pltpu.HBM)] * n


FAR = pltpu.HBM


def near(*arrays):
    return [pltpu.with_memory_space_constraint(v, pltpu.VMEM) for v in arrays]


def far(*arrays):
    return [pltpu.with_memory_space_constraint(v, pltpu.HBM) for v in arrays]


def sum_a_kernel(a0, a1, a2, a3, out, own, sem):
    copy = pltpu.make_async_copy(a0, own, sem)
    copy.start()
    copy.wait()
    out[...] = own[...] + a1[...] + a2[...] + a3[...]


def sum_b_kernel(*refs):
    first, rest, outs, own, sem = refs[0], refs[1:NZ], refs[NZ:-2], refs[-2], refs[-1]
    x = lax.axis_index("x")
    copy = pltpu.make_async_copy(first, own, sem)
    copy.start()
    copy.wait()
    for j, out in enumerate(outs):
        at = lax.rem(x + j, NX)
        total = own[at]
        for b in rest:
            total = total + b[at]
        out[...] = total


def step_kernel(a, b0, b1, b2, b3, weight, norm_weight, out, stepped, stepped_norm):
    rate = (NZ * NX * NC) ** (-0.5)
    total_a = a[0]
    for z in range(1, NZ):
        total_a = total_a + a[z]
    total_b = b0[...] + b1[...] + b2[...] + b3[...]
    for pieces, total in ((B_PIECES, total_b), (A_PIECES, total_a)):
        for t, low, high, at in pieces:
            lanes, place = slice(LANES * t, LANES * t + LANES), slice(at, at + high - low)
            stepped[low:high, lanes] = weight[low:high, lanes] - learn_rate * (total[place] * rate)
    stepped_norm[...] = norm_weight[...] - learn_rate * (total_b[B_ROWS - 8 :] * rate)
    for t in range(COLS):
        new = stepped[:, LANES * t : LANES * t + LANES].astype(bf16)
        for z in range(NZ):
            out[z, ROWS * t : ROWS * t + ROWS] = new
    new = stepped_norm[...].astype(bf16)
    for z in range(NZ):
        out[z, G_ROWS - 8 :] = new


def turn_kernel(own, a0, a1, a2, a3, *refs):
    q, k, v, m, turned, pair, sems = refs[-7:]
    core, x = lax.axis_index("c"), lax.axis_index("x")
    pairs = ((q, k), (v, m))

    def copies(i, pair_out):
        lanes = HALVES[i]
        return [
            pltpu.make_async_copy(pair.at[pl.ds(320 * j, 320), lanes], out.at[:, lanes], sems.at[i, j])
            for j, out in enumerate(pair_out)
        ]

    for i in range(2):
        for j, a in enumerate((a0, a1, a2, a3)):
            place = lax.rem(x + NX - j, NX) * ROWS
            for z in range(4):
                rows = pl.ds(pl.multiple_of(place + z * NX * ROWS, 8), ROWS)
                for t in range(COLS):
                    tile = a[4 * i + z, ROWS * t : ROWS * t + ROWS, :]
                    turned[rows, LANES * t : LANES * t + LANES] = tile.astype(f32)
        for t in range(COLS):
            lanes = slice(LANES * t, LANES * t + LANES)
            pair[lanes, 640 * i : 640 * i + 640] = turned[:, lanes].T.astype(bf16)
        for flip in range(2):

            @pl.when(core == (flip if own else 1 - flip))
            def _(flip=flip):
                for c in copies(i, pairs[flip]):
                    c.start()

    for i in range(2):
        for c in copies(i, pairs[0]):
            c.wait()


def call(kernel, out_shape, in_specs, scratch=(), out_specs=None, aliases={}):
    return pl.pallas_call(
        kernel,
        compiler_params=pltpu.CompilerParams(vmem_limit_bytes=24 << 20),
        out_shape=out_shape,
        in_specs=in_specs,
        out_specs=out_specs or jax.tree.map(lambda _: vmem(1)[0], out_shape),
        input_output_aliases=aliases,
        scratch_shapes=scratch,
    )


def on_device(pq, pk, pv, pm, pn, mq, mk, mv, mm, mn):
    core, x = lax.axis_index("c"), lax.axis_index("x")
    even = core == 0
    pq, pk, pv, pm = pq[0].T, pk[0].T, pv[0].T, pm[0]
    dma = pltpu.SemaphoreType.DMA

    norm = shift(pn, 0, 0, 1)
    norm = pn + norm
    norm = jnp.pad(norm.reshape(NZ, NX, 1, ROWS), ((0, 0), (0, 0), (0, 7), (0, LANES - ROWS)))
    chunks_b, chunks_a = SPLIT // CHUNK, (640 - SPLIT) // CHUNK
    send_b = call(
        pick_kernel, pltpu.VMEM((SPLIT, 1280), f32), hbm(2), [dma((chunks_b,))]
    )(*far(pq, pv))
    got_b = shift(send_b, 0, 0, 1)
    send_a = call(
        pick_kernel, pltpu.VMEM((640 - SPLIT, 1280), f32), hbm(4), [dma((chunks_a,))]
    )(*far(pq, pk, pv, pm))
    got_a = shift(send_a, 0, 0, 1)
    heads, tails = jnp.concatenate([mq, mk], 1), jnp.concatenate([mv, mm.T], 1)
    mine, theirs = jnp.where(even, heads, tails), shift(jnp.where(even, tails, heads), 0, 0, 1)
    weight = jnp.where(even, jnp.concatenate([mine, theirs]), jnp.concatenate([theirs, mine]))
    other = shift(mn, 0, 0, 1)
    norm_weight = jnp.where(even, jnp.concatenate([mn, other]), jnp.concatenate([other, mn]))
    norm_weight = jnp.pad(norm_weight[None], ((0, 7), (0, LANES - ROWS)))

    a_shape, b_shape = (NZ, A_ROWS, LANES), (NX, B_ROWS, LANES)
    *b, extra = call(
        split_b_kernel,
        [FAR(b_shape, f32)] * NZ + [pltpu.VMEM((NZ, NX, ROWS - EXTRA, LANES), f32)],
        hbm(2) + vmem(2),
        [pltpu.VMEM((SPLIT, 1280), f32), pltpu.VMEM((NZ, *b_shape), f32), dma((2, chunks_b)), dma((NZ,))],
        hbm(NZ) + vmem(1),
    )(*far(pq, pv), *near(got_b, norm))
    got = [b[0]]
    for steps in ((3, 5), (2, 6, 4, 1, 7)):
        got += [shift(b[r], r, 0) for r in steps]
    b = got
    a = call(
        split_a_kernel,
        [FAR(a_shape, f32)] + [pltpu.VMEM(a_shape, f32)] * 3,
        hbm(4) + vmem(2),
        [
            pltpu.VMEM((640 - SPLIT, 1280), f32),
            pltpu.VMEM((4, NX, ROWS, LANES), f32),
            dma((2, chunks_a)),
        ],
    )(*far(pq, pk, pv, pm), *near(got_a, extra))
    a = shift_x(a)
    a, b, weight, norm_weight = lax.optimization_barrier((a, b, weight, norm_weight))
    a = call(
        sum_a_kernel, pltpu.VMEM(a_shape, f32), hbm(1) + vmem(3), [pltpu.VMEM(a_shape, f32), dma]
    )(*far(a[0]), *near(*a[1:]))
    a = spread(a)
    b = call(
        sum_b_kernel,
        [pltpu.VMEM((B_ROWS, LANES), f32)] * NX,
        hbm(1) + vmem(NZ - 1),
        [pltpu.VMEM(b_shape, f32), dma],
    )(*far(b[0]), *near(*b[1:]))
    b = [b[0]] + [shift(b[j], 0, j) for j in (1, 2, 3)]
    a, stepped, stepped_norm = call(
        step_kernel,
        [
            pltpu.VMEM((NZ, G_ROWS, LANES), bf16),
            pltpu.VMEM((ROWS, 640), f32),
            pltpu.VMEM((8, LANES), f32),
        ],
        vmem(7),
    )(*near(a, *b, weight, norm_weight))

    a = spread(a)
    a = shift_x([a] * NX)
    stepped_norm = lax.dynamic_slice_in_dim(stepped_norm[0], 20 * core, 20)
    kept = lax.dynamic_slice_in_dim(stepped, 20 * core, 20)
    swapped = shift(lax.dynamic_slice_in_dim(stepped, 20 * (1 - core), 20), 0, 0, 1)
    heads, tails = jnp.where(even, kept, swapped), jnp.where(even, swapped, kept)
    outs = (heads[:, :320], heads[:, 320:], tails[:, :320], tails[:, 320:].T, stepped_norm)
    a[3], outs = lax.optimization_barrier((a[3], outs))
    other_a = [shift(v, 0, 0, 1) for v in a]
    own_x = jnp.arange(NX)[:, None]
    norm = sum(
        jnp.where(own_x == lax.rem(x + NX - j, NX), v[:, None, G_ROWS - 8, :ROWS], 0) for j, v in enumerate(a)
    )
    scratch = [pltpu.VMEM((640, 640), f32), pltpu.VMEM((640, 1280), bf16), dma((2, 2))]
    outs_shape = [FAR((320, 1280), bf16)] * 4
    half = call(partial(turn_kernel, True), outs_shape, vmem(4), scratch, hbm(4))(*near(*a))
    aliases = {4 + i: i for i in range(4)}
    q, k, v, m = call(
        partial(turn_kernel, False), outs_shape, vmem(4) + hbm(4), scratch, hbm(4), aliases
    )(*near(*other_a), *half)
    return (q.T, k.T, v.T, m, norm.reshape(-1).astype(bf16), *outs)


def solution(mesh):
    split = Mesh(mesh.devices.reshape(NZ, NX, NC, -1), ("z", "x", "c", "model"))
    r = CHIPS
    in_specs = (
        (P(r, None, "model"),) * 3
        + (P(r, "model", None), P(r, None))
        + (P(r, "model"),) * 3
        + (P("model", r), P(r))
    )
    out_specs = (
        (P(None, "model"),) * 3
        + (P("model", None), P())
        + (P(r, "model"),) * 3
        + (P("model", r), P(r))
    )
    return jax.shard_map(
        on_device, mesh=split, in_specs=in_specs, out_specs=out_specs, check_vma=False
    )
```

profile of v0, /device:TPU:1, one launch (start us, length us, event | category | flops | bytes accessed | tf_op | source)
XLA Modules:
  0.0 130.0 jit_solution(14610253735957944322)
XLA Ops:
  0.6 3.0 %shard_map.177 = f32[384,1280]{1,0:T(8,128)} custom-call(f32[320,1280]{1,0:T(8,128)} %bitcast.32, f32[320,1280]{1,0:T(8,128)} %bitcast.40, f32[320,1280]{1,0:T(8,128)} %bitcast.36, f32[320,1280]{1,0:T(8,128)} %bitcast.42), custom_call_target="tpu_custom_call" | custom-call | tf_op jit(solution)/shard_map/pallas_call | solution.py:254
  3.7 3.3 %collective-permute-start = (f32[384,1280]{1,0:T(8,128)}, f32[384,1280]{1,0:T(8,128)S(1)}, u32[]{:S(2)}, u32[]{:S(2)}) collective-permute-start(f32[384,1280]{1,0:T(8,128)} %shard_map.177), channel_id=1, source_target_pairs={{0,4},{4,0},{8,12},{12,8},{16,20},{20,16},{24,28},{28,24},{32,36},... | collective-permute-start | bytes 5898248 | tf_op jit(solution)/shard_map/ppermute | solution.py:33
  7.0 2.5 %shard_map.178 = f32[256,1280]{1,0:T(8,128)} custom-call(f32[320,1280]{1,0:T(8,128)} %bitcast.33, f32[320,1280]{1,0:T(8,128)} %bitcast.37), custom_call_target="tpu_custom_call" | custom-call | tf_op jit(solution)/shard_map/pallas_call | solution.py:250
  10.2 2.6 %collective-permute-done.2 = f32[1,1280]{1,0:T(1,128)S(1)} collective-permute-done((f32[1,1280]{1,0:T(1,128)S(1)}, f32[1,1280]{1,0:T(1,128)S(1)}, u32[]{:S(2)}, u32[]{:S(2)}) %collective-permute-start.2) | collective-permute-done | bytes 5152 | tf_op jit(solution)/shard_map/ppermute | solution.py:33
  13.0 2.9 %shard_map.179 = (f32[4,64,128]{2,1,0:T(8,128)}, f32[4,64,128]{2,1,0:T(8,128)}, f32[4,64,128]{2,1,0:T(8,128)}, f32[4,64,128]{2,1,0:T(8,128)}, f32[4,64,128]{2,1,...) custom-call(f32[320,1280]{1,0:T(8,128)} %bitcast.34, ...), custom_call_target="tpu_custom_call" | custom-call | tf_op jit(solution)/shard_map/pallas_call | solution.py:266
  15.9 2.7 %collective-permute-start.6 = (f32[4,64,128]{2,1,0:T(8,128)}, f32[4,64,128]{2,1,0:T(8,128)S(1)}, u32[]{:S(2)}, u32[]{:S(2)}) collective-permute-start(f32[4,64,128]{2,1,0:T(8,128)} %get-tuple-element.64), channel_id=1, source_target_pairs={{0,96},{4,100},{8,104},{12,108},{16,112},{20,116},{24,120},{28,124... | collective-permute-start | bytes 393224 | tf_op jit(solution)/shard_map/ppermute | solution.py:33
  18.7 3.5 %shard_map.180 = (f32[8,144,128]{2,1,0:T(8,128)}, f32[8,144,128]{2,1,0:T(8,128)S(1)}, f32[8,144,128]{2,1,0:T(8,128)S(1)}, f32[8,144,128]{2,1,0:T(8,128)S(1)}) custom-call(f32[320,1280]{1,0:T(8,128)} %bitcast.35, f32[320,1280]{1,0:T(8,128)} %bitcast.41, f32[320,1280]{1,0:T(8,128)} %bitcast.39, f32[320,1280]{1,0:T(8,128)} %bitcast.43, ...), custom_call_target="tpu_custom_call" | custom-call | tf_op jit(solution)/shard_map/pallas_call | solution.py:277
  23.5 2.5 %collective-permute-start.4 = (f32[8,144,128]{2,1,0:T(8,128)S(1)}, f32[8,144,128]{2,1,0:T(8,128)S(1)}, u32[]{:S(2)}, u32[]{:S(2)}) collective-permute-start(f32[8,144,128]{2,1,0:T(8,128)S(1)} %get-tuple-element.61), channel_id=1, source_target_pairs={{0,16},{4,20},{8,24},{12,28},{16,0},{20,4},{24,8},{28,12},{32,48},... | collective-permute-start | bytes 1769480 | tf_op jit(solution)/shard_map/ppermute | solution.py:33
  27.2 1.3 %collective-permute-start.13 = (f32[20,640]{1,0:T(8,128)S(1)}, f32[20,640]{1,0:T(8,128)S(1)}, u32[]{:S(2)}, u32[]{:S(2)}) collective-permute-start(f32[20,640]{1,0:T(8,128)S(1)} %get-tuple-element.109), channel_id=1, source_target_pairs={{0,4},{4,0},{8,12},{12,8},{16,20},{20,16},{24,28},{28,24},{32,36},... | collective-permute-start | bytes 153608 | tf_op jit(solution)/shard_map/ppermute | solution.py:33
  29.5 1.9 %collective-permute-start.7 = (f32[4,64,128]{2,1,0:T(8,128)S(1)}, f32[4,64,128]{2,1,0:T(8,128)S(1)}, u32[]{:S(2)}, u32[]{:S(2)}) collective-permute-start(f32[4,64,128]{2,1,0:T(8,128)S(1)} %copy-done.11), channel_id=1, source_target_pairs={{0,160},{4,164},{8,168},{12,172},{16,176},{20,180},{24,184},{28,18... | collective-permute-start | bytes 393224 | tf_op jit(solution)/shard_map/ppermute | solution.py:33
  31.3 1.5 %collective-permute-start.8 = (f32[4,64,128]{2,1,0:T(8,128)S(1)}, f32[4,64,128]{2,1,0:T(8,128)S(1)}, u32[]{:S(2)}, u32[]{:S(2)}) collective-permute-start(f32[4,64,128]{2,1,0:T(8,128)S(1)} %copy-done.10), channel_id=1, source_target_pairs={{0,64},{4,68},{8,72},{12,76},{16,80},{20,84},{24,88},{28,92},{32,9... | collective-permute-start | bytes 393224 | tf_op jit(solution)/shard_map/ppermute | solution.py:33
  32.9 4.0 %collective-permute-done.7.refs_2_ = f32[4,64,128]{2,1,0:T(8,128)S(1)} collective-permute-done((f32[4,64,128]{2,1,0:T(8,128)S(1)}, f32[4,64,128]{2,1,0:T(8,128)S(1)}, u32[]{:S(2)}, u32[]{:S(2)}) %collective-permute-start.7) | collective-permute-done | bytes 131104 | tf_op jit(solution)/shard_map/ppermute | solution.py:33
  36.9 7.9 %collective-permute-start.9 = (f32[4,64,128]{2,1,0:T(8,128)S(1)}, f32[4,64,128]{2,1,0:T(8,128)S(1)}, u32[]{:S(2)}, u32[]{:S(2)}) collective-permute-start(f32[4,64,128]{2,1,0:T(8,128)S(1)} %copy-done.9), channel_id=1, source_target_pairs={{0,192},{4,196},{8,200},{12,204},{16,208},{20,212},{24,216},{28,22... | collective-permute-start | bytes 393224 | tf_op jit(solution)/shard_map/ppermute | solution.py:33
  44.8 1.5 %collective-permute-start.10 = (f32[4,64,128]{2,1,0:T(8,128)S(1)}, f32[4,64,128]{2,1,0:T(8,128)S(1)}, u32[]{:S(2)}, u32[]{:S(2)}) collective-permute-start(f32[4,64,128]{2,1,0:T(8,128)S(1)} %copy-done.8), channel_id=1, source_target_pairs={{0,128},{4,132},{8,136},{12,140},{16,144},{20,148},{24,152},{28,15... | collective-permute-start | bytes 393224 | tf_op jit(solution)/shard_map/ppermute | solution.py:33
  46.2 3.8 %collective-permute-done.9.refs_4_ = f32[4,64,128]{2,1,0:T(8,128)S(1)} collective-permute-done((f32[4,64,128]{2,1,0:T(8,128)S(1)}, f32[4,64,128]{2,1,0:T(8,128)S(1)}, u32[]{:S(2)}, u32[]{:S(2)}) %collective-permute-start.9) | collective-permute-done | bytes 131104 | tf_op jit(solution)/shard_map/ppermute | solution.py:33
  50.5 5.9 %collective-permute-done.10.refs_5_ = f32[4,64,128]{2,1,0:T(8,128)S(1)} collective-permute-done((f32[4,64,128]{2,1,0:T(8,128)S(1)}, f32[4,64,128]{2,1,0:T(8,128)S(1)}, u32[]{:S(2)}, u32[]{:S(2)}) %collective-permute-start.10) | collective-permute-done | bytes 131104 | tf_op jit(solution)/shard_map/ppermute | solution.py:33
  57.2 4.8 %collective-permute-done.12.refs_7_ = f32[4,64,128]{2,1,0:T(8,128)S(1)} collective-permute-done((f32[4,64,128]{2,1,0:T(8,128)S(1)}, f32[4,64,128]{2,1,0:T(8,128)S(1)}, u32[]{:S(2)}, u32[]{:S(2)}) %collective-permute-start.12) | collective-permute-done | bytes 131104 | tf_op jit(solution)/shard_map/ppermute | solution.py:33
  62.0 2.0 %shard_map.181 = f32[8,144,128]{2,1,0:T(8,128)} custom-call(f32[8,144,128]{2,1,0:T(8,128)} %get-tuple-element.71.a0, f32[8,144,128]{2,1,0:T(8,128)S(1)} %collective-permute-done.3.a1, f32[8,144,128]{2,1,0:T(8,128)S(1)} %collective-permute-done.4.a2, f32[8,144,128]{2,1,0:T(8,128)S(1)} %collective-permute-done.5.a3), custom_call_target="tpu_custom_call" | custom-call | tf_op jit(solution)/shard_map/pallas_call | solution.py:289
  64.0 4.8 %all-to-all-start = ((f32[8,144,128]{2,1,0:T(8,128)}), f32[8,144,128]{2,1,0:T(8,128)S(1)}, u32[]{:S(2)}, u32[]{:S(2)}) async-start(f32[8,144,128]{2,1,0:T(8,128)} %shard_map.181), calls=%async_computation | async-start | bytes 1179648 | tf_op jit(solution)/shard_map/all_to_all | solution.py:42
  70.7 1.9 %collective-permute-start.17 = (f32[64,128]{1,0:T(8,128)S(1)}, f32[64,128]{1,0:T(8,128)S(1)}, u32[]{:S(2)}, u32[]{:S(2)}) collective-permute-start(f32[64,128]{1,0:T(8,128)S(1)} %get-tuple-element.86), channel_id=1, source_target_pairs={{0,24},{4,28},{8,0},{12,4},{16,8},{20,12},{24,16},{28,20},{32,56},... | collective-permute-start | bytes 98312 | tf_op jit(solution)/shard_map/ppermute | solution.py:33
  75.0 10.7 %all-to-all-done.a = f32[8,144,128]{2,1,0:T(8,128)S(1)} async-done(((f32[8,144,128]{2,1,0:T(8,128)}), f32[8,144,128]{2,1,0:T(8,128)S(1)}, u32[]{:S(2)}, u32[]{:S(2)}) %all-to-all-start) | async-done | bytes 589856 | tf_op jit(solution)/shard_map/all_to_all | solution.py:42
  86.5 3.5 %all-to-all-start.1 = ((bf16[8,208,128]{2,1,0:T(8,128)(2,1)}), bf16[8,208,128]{2,1,0:T(8,128)(2,1)S(1)}, u32[]{:S(2)}, u32[]{:S(2)}) async-start(bf16[8,208,128]{2,1,0:T(8,128)(2,1)} %get-tuple-element.89), calls=%async_computation.1 | async-start | bytes 851968 | tf_op jit(solution)/shard_map/all_to_all | solution.py:42
  90.1 3.0 %collective-permute-start.24 = (f32[20,640]{1,0:T(8,128)S(1)}, f32[20,640]{1,0:T(8,128)S(1)}, u32[]{:S(2)}, u32[]{:S(2)}) collective-permute-start(f32[20,640]{1,0:T(8,128)S(1)} %constant_dynamic-slice_fusion.1), channel_id=1, source_target_pairs={{0,4},{4,0},{8,12},{12,8},{16,20},{20,16},{24,28},{28,24},{32,36},... | collective-permute-start | bytes 153608 | tf_op jit(solution)/shard_map/ppermute | solution.py:33
  93.6 8.5 %all-to-all-done.1.a0 = bf16[8,208,128]{2,1,0:T(8,128)(2,1)S(1)} async-done(((bf16[8,208,128]{2,1,0:T(8,128)(2,1)}), bf16[8,208,128]{2,1,0:T(8,128)(2,1)S(1)}, u32[]{:S(2)}, u32[]{:S(2)}) %all-to-all-start.1) | async-done | bytes 426016 | tf_op jit(solution)/shard_map/all_to_all | solution.py:42
  102.1 2.1 %collective-permute-start.21 = (bf16[8,208,128]{2,1,0:T(8,128)(2,1)S(1)}, bf16[8,208,128]{2,1,0:T(8,128)(2,1)S(1)}, u32[]{:S(2)}, u32[]{:S(2)}) collective-permute-start(bf16[8,208,128]{2,1,0:T(8,128)(2,1)S(1)} %all-to-all-done.1.a0), channel_id=1, source_target_pairs={{0,16},{4,20},{8,24},{12,28},{16,0},{20,4},{24,8},{28,12},{32,48},... | collective-permute-start | bytes 1277960 | tf_op jit(solution)/shard_map/ppermute | solution.py:33
  105.0 4.7 %collective-permute-start.18 = (bf16[8,208,128]{2,1,0:T(8,128)(2,1)S(1)}, bf16[8,208,128]{2,1,0:T(8,128)(2,1)S(1)}, u32[]{:S(2)}, u32[]{:S(2)}) collective-permute-start(bf16[8,208,128]{2,1,0:T(8,128)(2,1)S(1)} %all-to-all-done.1.a0), channel_id=1, source_target_pairs={{0,4},{4,0},{8,12},{12,8},{16,20},{20,16},{24,28},{28,24},{32,36},... | collective-permute-start | bytes 1277960 | tf_op jit(solution)/shard_map/ppermute | solution.py:33
  109.7 9.2 %collective-permute-start.25 = (bf16[8,208,128]{2,1,0:T(8,128)(2,1)S(1)}, bf16[8,208,128]{2,1,0:T(8,128)(2,1)S(1)}, u32[]{:S(2)}, u32[]{:S(2)}) collective-permute-start(bf16[8,208,128]{2,1,0:T(8,128)(2,1)S(1)} %collective-permute-done.23.a3), channel_id=1, source_target_pairs={{0,4},{4,0},{8,12},{12,8},{16,20},{20,16},{24,28},{28,24},{32,36},... | collective-permute-start | bytes 1277960 | tf_op jit(solution)/shard_map/ppermute | solution.py:33
  118.9 1.5 %collective-permute-start.22 = (bf16[8,208,128]{2,1,0:T(8,128)(2,1)S(1)}, bf16[8,208,128]{2,1,0:T(8,128)(2,1)S(1)}, u32[]{:S(2)}, u32[]{:S(2)}) collective-permute-start(bf16[8,208,128]{2,1,0:T(8,128)(2,1)S(1)} %collective-permute-done.21.a2), channel_id=1, source_target_pairs={{0,4},{4,0},{8,12},{12,8},{16,20},{20,16},{24,28},{28,24},{32,36},... | collective-permute-start | bytes 1277960 | tf_op jit(solution)/shard_map/ppermute | solution.py:33
  120.5 2.9 %collective-permute-done.19.a1 = bf16[8,208,128]{2,1,0:T(8,128)(2,1)S(1)} collective-permute-done((bf16[8,208,128]{2,1,0:T(8,128)(2,1)S(1)}, bf16[8,208,128]{2,1,0:T(8,128)(2,1)S(1)}, u32[]{:S(2)}, u32[]{:S(2)}) %collective-permute-start.19) | collective-permute-done | bytes 426016 | tf_op jit(solution)/shard_map/ppermute | solution.py:33
  123.3 1.6 %collective-permute-start.20 = (bf16[8,208,128]{2,1,0:T(8,128)(2,1)S(1)}, bf16[8,208,128]{2,1,0:T(8,128)(2,1)S(1)}, u32[]{:S(2)}, u32[]{:S(2)}) collective-permute-start(bf16[8,208,128]{2,1,0:T(8,128)(2,1)S(1)} %collective-permute-done.19.a1), channel_id=1, source_target_pairs={{0,4},{4,0},{8,12},{12,8},{16,20},{20,16},{24,28},{28,24},{32,36},... | collective-permute-start | bytes 1277960 | tf_op jit(solution)/shard_map/ppermute | solution.py:33
  125.9 2.0 %shard_map.184 = (bf16[320,1280]{1,0:T(8,128)(2,1)}, bf16[320,1280]{1,0:T(8,128)(2,1)}, bf16[320,1280]{1,0:T(8,128)(2,1)}, bf16[320,1280]{1,0:T(8,128)(2,1)}) custom-call(bf16[8,208,128]{2,1,0:T(8,128)(2,1)S(1)} %all-to-all-done.1.a0, bf16[8,208,128]{2,1,0:T(8,128)(2,1)S(1)} %collective-permute-done.19.a1, ...), custom_call_target="tpu_custom_call" | custom-call | tf_op jit(solution)/shard_map/pallas_call | solution.py:325
  127.9 2.0 %shard_map.185 = (bf16[320,1280]{1,0:T(8,128)(2,1)}, bf16[320,1280]{1,0:T(8,128)(2,1)}, bf16[320,1280]{1,0:T(8,128)(2,1)}, bf16[320,1280]{1,0:T(8,128)(2,1)}) custom-call(bf16[8,208,128]{2,1,0:T(8,128)(2,1)S(1)} %collective-permute-done.18.a0, ...), custom_call_target="tpu_custom_call", output_to_operand_aliasing={{0}: (4, {}), {1}: (5, {}), {2}: (6, {}), {3}: (7, {})} | custom-call | tf_op jit(solution)/shard_map/pallas_call | solution.py:327
  (81 shorter events, 12.9 us)
Async XLA Ops:
  3.7 14.9 %collective-permute-start = (f32[384,1280]{1,0:T(8,128)}, f32[384,1280]{1,0:T(8,128)S(1)}, u32[]{:S(2)}, u32[]{:S(2)}) collective-permute-start(f32[384,1280]{1,0:T(8,128)} %shard_map.177), channel_id=1, source_target_pairs={{0,4},{4,0},{8,12},{12,8},{16,20},{20,16},{24,28},{28,24},{32,36},... | collective-permute-start | bytes 5898248 | tf_op jit(solution)/shard_map/ppermute | solution.py:33
  9.5 3.5 %collective-permute-start.1 = (f32[256,1280]{1,0:T(8,128)}, f32[256,1280]{1,0:T(8,128)S(1)}, u32[]{:S(2)}, u32[]{:S(2)}) collective-permute-start(f32[256,1280]{1,0:T(8,128)} %shard_map.178), channel_id=1, source_target_pairs={{0,4},{4,0},{8,12},{12,8},{16,20},{20,16},{24,28},{28,24},{32,36},... | collective-permute-start | bytes 3932168 | tf_op jit(solution)/shard_map/ppermute | solution.py:33
  9.6 3.2 %collective-permute-start.2 = (f32[1,1280]{1,0:T(1,128)S(1)}, f32[1,1280]{1,0:T(1,128)S(1)}, u32[]{:S(2)}, u32[]{:S(2)}) collective-permute-start(f32[1,1280]{1,0:T(1,128)S(1)} %copy-done.4), channel_id=1, source_target_pairs={{0,4},{4,0},{8,12},{12,8},{16,20},{20,16},{24,28},{28,24},{32,36},... | collective-permute-start | bytes 15368 | tf_op jit(solution)/shard_map/ppermute | solution.py:33
  10.1 17.1 %collective-permute-start.14 = (f32[20]{0:T(128)S(1)}, f32[20]{0:T(128)S(1)}, u32[]{:S(2)}, u32[]{:S(2)}) collective-permute-start(f32[20]{0:T(128)S(1)} %copy-done.5), channel_id=1, source_target_pairs={{0,4},{4,0},{8,12},{12,8},{16,20},{20,16},{24,28},{28,24},{32,36},... | collective-permute-start | bytes 248 | tf_op jit(solution)/shard_map/ppermute | solution.py:33
  15.9 15.4 %collective-permute-start.6 = (f32[4,64,128]{2,1,0:T(8,128)}, f32[4,64,128]{2,1,0:T(8,128)S(1)}, u32[]{:S(2)}, u32[]{:S(2)}) collective-permute-start(f32[4,64,128]{2,1,0:T(8,128)} %get-tuple-element.64), channel_id=1, source_target_pairs={{0,96},{4,100},{8,104},{12,108},{16,112},{20,116},{24,120},{28,124... | collective-permute-start | bytes 393224 | tf_op jit(solution)/shard_map/ppermute | solution.py:33
  18.7 18.2 %copy-start.9 = (f32[4,64,128]{2,1,0:T(8,128)S(1)}, f32[4,64,128]{2,1,0:T(8,128)}, u32[]{:S(2)}) copy-start(f32[4,64,128]{2,1,0:T(8,128)} %get-tuple-element.67) | copy-start | bytes 393220
  18.7 26.1 %copy-start.8 = (f32[4,64,128]{2,1,0:T(8,128)S(1)}, f32[4,64,128]{2,1,0:T(8,128)}, u32[]{:S(2)}) copy-start(f32[4,64,128]{2,1,0:T(8,128)} %get-tuple-element.68) | copy-start | bytes 393220
  18.7 31.4 %copy-start.7 = (f32[4,64,128]{2,1,0:T(8,128)S(1)}, f32[4,64,128]{2,1,0:T(8,128)}, u32[]{:S(2)}) copy-start(f32[4,64,128]{2,1,0:T(8,128)} %get-tuple-element.69) | copy-start | bytes 393220
  18.7 37.7 %copy-start.6 = (f32[4,64,128]{2,1,0:T(8,128)S(1)}, f32[4,64,128]{2,1,0:T(8,128)}, u32[]{:S(2)}) copy-start(f32[4,64,128]{2,1,0:T(8,128)} %get-tuple-element.70) | copy-start | bytes 393220
  22.2 39.8 %collective-permute-start.3 = (f32[8,144,128]{2,1,0:T(8,128)S(1)}, f32[8,144,128]{2,1,0:T(8,128)S(1)}, u32[]{:S(2)}, u32[]{:S(2)}) collective-permute-start(f32[8,144,128]{2,1,0:T(8,128)S(1)} %get-tuple-element.60), channel_id=1, source_target_pairs={{0,8},{4,12},{8,16},{12,20},{16,24},{20,28},{24,0},{28,4},{32,40},... | collective-permute-start | bytes 1769480 | tf_op jit(solution)/shard_map/ppermute | solution.py:33
  23.5 38.5 %collective-permute-start.4 = (f32[8,144,128]{2,1,0:T(8,128)S(1)}, f32[8,144,128]{2,1,0:T(8,128)S(1)}, u32[]{:S(2)}, u32[]{:S(2)}) collective-permute-start(f32[8,144,128]{2,1,0:T(8,128)S(1)} %get-tuple-element.61), channel_id=1, source_target_pairs={{0,16},{4,20},{8,24},{12,28},{16,0},{20,4},{24,8},{28,12},{32,48},... | collective-permute-start | bytes 1769480 | tf_op jit(solution)/shard_map/ppermute | solution.py:33
  26.0 36.0 %collective-permute-start.5 = (f32[8,144,128]{2,1,0:T(8,128)S(1)}, f32[8,144,128]{2,1,0:T(8,128)S(1)}, u32[]{:S(2)}, u32[]{:S(2)}) collective-permute-start(f32[8,144,128]{2,1,0:T(8,128)S(1)} %get-tuple-element.62), channel_id=1, source_target_pairs={{0,24},{4,28},{8,0},{12,4},{16,8},{20,12},{24,16},{28,20},{32,56},... | collective-permute-start | bytes 1769480 | tf_op jit(solution)/shard_map/ppermute | solution.py:33
  27.2 2.2 %collective-permute-start.13 = (f32[20,640]{1,0:T(8,128)S(1)}, f32[20,640]{1,0:T(8,128)S(1)}, u32[]{:S(2)}, u32[]{:S(2)}) collective-permute-start(f32[20,640]{1,0:T(8,128)S(1)} %get-tuple-element.109), channel_id=1, source_target_pairs={{0,4},{4,0},{8,12},{12,8},{16,20},{20,16},{24,28},{28,24},{32,36},... | collective-permute-start | bytes 153608 | tf_op jit(solution)/shard_map/ppermute | solution.py:33
  29.5 7.4 %collective-permute-start.7 = (f32[4,64,128]{2,1,0:T(8,128)S(1)}, f32[4,64,128]{2,1,0:T(8,128)S(1)}, u32[]{:S(2)}, u32[]{:S(2)}) collective-permute-start(f32[4,64,128]{2,1,0:T(8,128)S(1)} %copy-done.11), channel_id=1, source_target_pairs={{0,160},{4,164},{8,168},{12,172},{16,176},{20,180},{24,184},{28,18... | collective-permute-start | bytes 393224 | tf_op jit(solution)/shard_map/ppermute | solution.py:33
  31.3 13.4 %collective-permute-start.8 = (f32[4,64,128]{2,1,0:T(8,128)S(1)}, f32[4,64,128]{2,1,0:T(8,128)S(1)}, u32[]{:S(2)}, u32[]{:S(2)}) collective-permute-start(f32[4,64,128]{2,1,0:T(8,128)S(1)} %copy-done.10), channel_id=1, source_target_pairs={{0,64},{4,68},{8,72},{12,76},{16,80},{20,84},{24,88},{28,92},{32,9... | collective-permute-start | bytes 393224 | tf_op jit(solution)/shard_map/ppermute | solution.py:33
  36.9 13.2 %collective-permute-start.9 = (f32[4,64,128]{2,1,0:T(8,128)S(1)}, f32[4,64,128]{2,1,0:T(8,128)S(1)}, u32[]{:S(2)}, u32[]{:S(2)}) collective-permute-start(f32[4,64,128]{2,1,0:T(8,128)S(1)} %copy-done.9), channel_id=1, source_target_pairs={{0,192},{4,196},{8,200},{12,204},{16,208},{20,212},{24,216},{28,22... | collective-permute-start | bytes 393224 | tf_op jit(solution)/shard_map/ppermute | solution.py:33
  44.8 11.6 %collective-permute-start.10 = (f32[4,64,128]{2,1,0:T(8,128)S(1)}, f32[4,64,128]{2,1,0:T(8,128)S(1)}, u32[]{:S(2)}, u32[]{:S(2)}) collective-permute-start(f32[4,64,128]{2,1,0:T(8,128)S(1)} %copy-done.8), channel_id=1, source_target_pairs={{0,128},{4,132},{8,136},{12,140},{16,144},{20,148},{24,152},{28,15... | collective-permute-start | bytes 393224 | tf_op jit(solution)/shard_map/ppermute | solution.py:33
  50.0 7.1 %collective-permute-start.11 = (f32[4,64,128]{2,1,0:T(8,128)S(1)}, f32[4,64,128]{2,1,0:T(8,128)S(1)}, u32[]{:S(2)}, u32[]{:S(2)}) collective-permute-start(f32[4,64,128]{2,1,0:T(8,128)S(1)} %copy-done.7), channel_id=1, source_target_pairs={{0,32},{4,36},{8,40},{12,44},{16,48},{20,52},{24,56},{28,60},{32,6... | collective-permute-start | bytes 393224 | tf_op jit(solution)/shard_map/ppermute | solution.py:33
  56.4 5.5 %collective-permute-start.12 = (f32[4,64,128]{2,1,0:T(8,128)S(1)}, f32[4,64,128]{2,1,0:T(8,128)S(1)}, u32[]{:S(2)}, u32[]{:S(2)}) collective-permute-start(f32[4,64,128]{2,1,0:T(8,128)S(1)} %copy-done.6), channel_id=1, source_target_pairs={{0,224},{4,228},{8,232},{12,236},{16,240},{20,244},{24,248},{28,25... | collective-permute-start | bytes 393224 | tf_op jit(solution)/shard_map/ppermute | solution.py:33
  64.0 21.7 %all-to-all-start = ((f32[8,144,128]{2,1,0:T(8,128)}), f32[8,144,128]{2,1,0:T(8,128)S(1)}, u32[]{:S(2)}, u32[]{:S(2)}) async-start(f32[8,144,128]{2,1,0:T(8,128)} %shard_map.181), calls=%async_computation | async-start | bytes 1179648 | tf_op jit(solution)/shard_map/all_to_all | solution.py:42
  69.7 4.1 %collective-permute-start.15 = (f32[64,128]{1,0:T(8,128)S(1)}, f32[64,128]{1,0:T(8,128)S(1)}, u32[]{:S(2)}, u32[]{:S(2)}) collective-permute-start(f32[64,128]{1,0:T(8,128)S(1)} %get-tuple-element.84), channel_id=1, source_target_pairs={{0,8},{4,12},{8,16},{12,20},{16,24},{20,28},{24,0},{28,4},{32,40},... | collective-permute-start | bytes 98312 | tf_op jit(solution)/shard_map/ppermute | solution.py:33
  70.1 4.3 %collective-permute-start.16 = (f32[64,128]{1,0:T(8,128)S(1)}, f32[64,128]{1,0:T(8,128)S(1)}, u32[]{:S(2)}, u32[]{:S(2)}) collective-permute-start(f32[64,128]{1,0:T(8,128)S(1)} %get-tuple-element.85), channel_id=1, source_target_pairs={{0,16},{4,20},{8,24},{12,28},{16,0},{20,4},{24,8},{28,12},{32,48},... | collective-permute-start | bytes 98312 | tf_op jit(solution)/shard_map/ppermute | solution.py:33
  70.7 4.3 %collective-permute-start.17 = (f32[64,128]{1,0:T(8,128)S(1)}, f32[64,128]{1,0:T(8,128)S(1)}, u32[]{:S(2)}, u32[]{:S(2)}) collective-permute-start(f32[64,128]{1,0:T(8,128)S(1)} %get-tuple-element.86), channel_id=1, source_target_pairs={{0,24},{4,28},{8,0},{12,4},{16,8},{20,12},{24,16},{28,20},{32,56},... | collective-permute-start | bytes 98312 | tf_op jit(solution)/shard_map/ppermute | solution.py:33
  86.5 15.6 %all-to-all-start.1 = ((bf16[8,208,128]{2,1,0:T(8,128)(2,1)}), bf16[8,208,128]{2,1,0:T(8,128)(2,1)S(1)}, u32[]{:S(2)}, u32[]{:S(2)}) async-start(bf16[8,208,128]{2,1,0:T(8,128)(2,1)} %get-tuple-element.89), calls=%async_computation.1 | async-start | bytes 851968 | tf_op jit(solution)/shard_map/all_to_all | solution.py:42
  90.1 14.2 %collective-permute-start.24 = (f32[20,640]{1,0:T(8,128)S(1)}, f32[20,640]{1,0:T(8,128)S(1)}, u32[]{:S(2)}, u32[]{:S(2)}) collective-permute-start(f32[20,640]{1,0:T(8,128)S(1)} %constant_dynamic-slice_fusion.1), channel_id=1, source_target_pairs={{0,4},{4,0},{8,12},{12,8},{16,20},{20,16},{24,28},{28,24},{32,36},... | collective-permute-start | bytes 153608 | tf_op jit(solution)/shard_map/ppermute | solution.py:33
  102.1 7.6 %collective-permute-start.23 = (bf16[8,208,128]{2,1,0:T(8,128)(2,1)S(1)}, bf16[8,208,128]{2,1,0:T(8,128)(2,1)S(1)}, u32[]{:S(2)}, u32[]{:S(2)}) collective-permute-start(bf16[8,208,128]{2,1,0:T(8,128)(2,1)S(1)} %all-to-all-done.1.a0), channel_id=1, source_target_pairs={{0,24},{4,28},{8,0},{12,4},{16,8},{20,12},{24,16},{28,20},{32,56},... | collective-permute-start | bytes 1277960 | tf_op jit(solution)/shard_map/ppermute | solution.py:33
  102.1 16.8 %collective-permute-start.21 = (bf16[8,208,128]{2,1,0:T(8,128)(2,1)S(1)}, bf16[8,208,128]{2,1,0:T(8,128)(2,1)S(1)}, u32[]{:S(2)}, u32[]{:S(2)}) collective-permute-start(bf16[8,208,128]{2,1,0:T(8,128)(2,1)S(1)} %all-to-all-done.1.a0), channel_id=1, source_target_pairs={{0,16},{4,20},{8,24},{12,28},{16,0},{20,4},{24,8},{28,12},{32,48},... | collective-permute-start | bytes 1277960 | tf_op jit(solution)/shard_map/ppermute | solution.py:33
  104.2 19.1 %collective-permute-start.19 = (bf16[8,208,128]{2,1,0:T(8,128)(2,1)S(1)}, bf16[8,208,128]{2,1,0:T(8,128)(2,1)S(1)}, u32[]{:S(2)}, u32[]{:S(2)}) collective-permute-start(bf16[8,208,128]{2,1,0:T(8,128)(2,1)S(1)} %all-to-all-done.1.a0), channel_id=1, source_target_pairs={{0,8},{4,12},{8,16},{12,20},{16,24},{20,28},{24,0},{28,4},{32,40},... | collective-permute-start | bytes 1277960 | tf_op jit(solution)/shard_map/ppermute | solution.py:33
  105.0 22.9 %collective-permute-start.18 = (bf16[8,208,128]{2,1,0:T(8,128)(2,1)S(1)}, bf16[8,208,128]{2,1,0:T(8,128)(2,1)S(1)}, u32[]{:S(2)}, u32[]{:S(2)}) collective-permute-start(bf16[8,208,128]{2,1,0:T(8,128)(2,1)S(1)} %all-to-all-done.1.a0), channel_id=1, source_target_pairs={{0,4},{4,0},{8,12},{12,8},{16,20},{20,16},{24,28},{28,24},{32,36},... | collective-permute-start | bytes 1277960 | tf_op jit(solution)/shard_map/ppermute | solution.py:33
  109.7 18.2 %collective-permute-start.25 = (bf16[8,208,128]{2,1,0:T(8,128)(2,1)S(1)}, bf16[8,208,128]{2,1,0:T(8,128)(2,1)S(1)}, u32[]{:S(2)}, u32[]{:S(2)}) collective-permute-start(bf16[8,208,128]{2,1,0:T(8,128)(2,1)S(1)} %collective-permute-done.23.a3), channel_id=1, source_target_pairs={{0,4},{4,0},{8,12},{12,8},{16,20},{20,16},{24,28},{28,24},{32,36},... | collective-permute-start | bytes 1277960 | tf_op jit(solution)/shard_map/ppermute | solution.py:33
  118.9 8.9 %collective-permute-start.22 = (bf16[8,208,128]{2,1,0:T(8,128)(2,1)S(1)}, bf16[8,208,128]{2,1,0:T(8,128)(2,1)S(1)}, u32[]{:S(2)}, u32[]{:S(2)}) collective-permute-start(bf16[8,208,128]{2,1,0:T(8,128)(2,1)S(1)} %collective-permute-done.21.a2), channel_id=1, source_target_pairs={{0,4},{4,0},{8,12},{12,8},{16,20},{20,16},{24,28},{28,24},{32,36},... | collective-permute-start | bytes 1277960 | tf_op jit(solution)/shard_map/ppermute | solution.py:33
  123.3 4.5 %collective-permute-start.20 = (bf16[8,208,128]{2,1,0:T(8,128)(2,1)S(1)}, bf16[8,208,128]{2,1,0:T(8,128)(2,1)S(1)}, u32[]{:S(2)}, u32[]{:S(2)}) collective-permute-start(bf16[8,208,128]{2,1,0:T(8,128)(2,1)S(1)} %collective-permute-done.19.a1), channel_id=1, source_target_pairs={{0,4},{4,0},{8,12},{12,8},{16,20},{20,16},{24,28},{28,24},{32,36},... | collective-permute-start | bytes 1277960 | tf_op jit(solution)/shard_map/ppermute | solution.py:33
  (8 other events, 69.8 us)
where the time goes:
time: 130 us
  starting transfers between devices  59.5 us (46%)
  waiting for transfers between devices  47.2 us (36%)
  Pallas kernels  19.6 us (15%)
  local copies, waits for them, and re-layouts  2.22 us (2%)
    ppermute x26, starting transfers between devices, shift(): return lax.ppermute(v, CHIPS, pairs)  51.2 us
    ppermute x26, waiting for transfers between devices, shift(): return lax.ppermute(v, CHIPS, pairs)  28 us
    all_to_all x2, waiting for transfers between devices, spread(): return lax.all_to_all(v, 'z', 0, 0, tiled=True)  19.2 us
    all_to_all x2, starting transfers between devices, spread(): return lax.all_to_all(v, 'z', 0, 0, tiled=True)  8.22 us
    pallas_call x1, Pallas kernels, on_device(): call(split_a_kernel, [FAR(a_shape, f32)] + [pltpu.VMEM(a_shape, f32)] * 3...  3.48 us
    pallas_call x1, Pallas kernels, on_device(): call(pick_kernel, pltpu.VMEM((640 - SPLIT, 1280), f32), hbm(4), [dma((chu...  3.03 us
    pallas_call x1, Pallas kernels, on_device(): call(split_b_kernel, [FAR(b_shape, f32)] * NZ + [pltpu.VMEM((NZ, NX, ROWS...  2.89 us
  transfers between devices with their start and end apart: 28, of which 13 were waited for; matrix products, arithmetic and copies ran while one was open for 2% of the time, Pallas kernels for 9%

commit v1 on v0

--- a/solution.py
+++ b/solution.py
@@ -13,14 +13,10 @@
 NZ, NX, NC = 8, 4, 2
 CHIPS = ("z", "x", "c")
 f32, bf16 = jnp.float32, jnp.bfloat16
-ROWS, LANES, COLS, EXTRA = 40, 128, 5, 16
-B_PIECES = ((0, 0, ROWS, 0), (1, 0, EXTRA, ROWS))
-A_PIECES = ((2, 0, ROWS, 0), (3, 0, ROWS, ROWS), (4, 0, ROWS, 2 * ROWS), (1, EXTRA, ROWS, 3 * ROWS))
-A_ROWS = 4 * ROWS - EXTRA
-B_ROWS = ROWS + EXTRA + 8
+ROWS, LANES, COLS = 40, 128, 5
+A_ROWS, B_ROWS, SPLIT = 4 * ROWS, ROWS + 8, LANES
 G_ROWS = COLS * ROWS + 8
 CHUNK = 32
-SPLIT = 2 * LANES
 
 
 def shift(v, dz, dx, dc=0):
@@ -83,7 +79,7 @@
 
 
 def split_b_kernel(q, v, got, norm, *refs):
-    *outs, extra, own, b, sems, out_sems = refs
+    *outs, own, b, sems, out_sems = refs
     z0 = lax.axis_index("z")
     pairs = blocks_b(q, v)
     halves = lambda blocks: [block_copies(blocks, own, sems.at[i], HALVES[i]) for i in range(2)]
@@ -92,19 +88,12 @@
     for z, step in enumerate(steps):
         b[step, :, B_ROWS - 8 :, :] = norm[z]
     for i, copies in enumerate(halves(pairs[0])):
-        lanes, some = slice(640 * i, 640 * i + 640), slice(4 * i, 4 * i + 4)
-        for t in range(2):
-            rows = slice(LANES * t, LANES * t + LANES)
-            for c in copies[LANES // CHUNK * t : LANES // CHUNK * (t + 1)]:
-                c.wait()
-            tile = (own[rows, lanes] + got[rows, lanes]).T.reshape(4, NX, ROWS, LANES)
-            for z in range(4):
-                if t == 0:
-                    b[steps[4 * i + z], :, :ROWS, :] = tile[z]
-                else:
-                    b[steps[4 * i + z], :, ROWS : ROWS + EXTRA, :] = tile[z, :, :EXTRA]
-            if t == 1:
-                extra[some] = tile[:, :, EXTRA:]
+        for c in copies:
+            c.wait()
+        lanes = slice(640 * i, 640 * i + 640)
+        tile = (own[:, lanes] + got[:, lanes]).T.reshape(4, NX, ROWS, LANES)
+        for z in range(4):
+            b[steps[4 * i + z], :, :ROWS, :] = tile[z]
     out_copies = [pltpu.make_async_copy(b.at[r], outs[r], out_sems.at[r]) for r in range(NZ)]
     for c in out_copies:
         c.start()
@@ -112,16 +101,14 @@
         c.wait()
 
 
-def split_a_kernel(q, k, v, m, got, extra, a0, a1, a2, a3, own, turned, sems):
+def split_a_kernel(q, k, v, m, got, a0, a1, a2, a3, own, turned, sems):
     x = lax.axis_index("x")
     pairs = blocks_a(q, k, v, m)
     halves = lambda blocks: [block_copies(blocks, own, sems.at[i], HALVES[i]) for i in range(2)]
     start_for(lambda core: core, pairs, lambda blocks: sum(halves(blocks), []))
-    for j, a in enumerate((a0, a1, a2, a3)):
-        a[:, 3 * ROWS :, :] = extra[:, lax.rem(x + j, NX)]
     for i, copies in enumerate(halves(pairs[0])):
         lanes = slice(640 * i, 640 * i + 640)
-        for t in range(3):
+        for t in range(COLS - 1):
             rows = slice(LANES * t, LANES * t + LANES)
             for c in copies[LANES // CHUNK * t : LANES // CHUNK * (t + 1)]:
                 c.wait()
@@ -176,10 +163,10 @@
     for z in range(1, NZ):
         total_a = total_a + a[z]
     total_b = b0[...] + b1[...] + b2[...] + b3[...]
-    for pieces, total in ((B_PIECES, total_b), (A_PIECES, total_a)):
-        for t, low, high, at in pieces:
-            lanes, place = slice(LANES * t, LANES * t + LANES), slice(at, at + high - low)
-            stepped[low:high, lanes] = weight[low:high, lanes] - learn_rate * (total[place] * rate)
+    for t in range(COLS):
+        lanes = slice(LANES * t, LANES * t + LANES)
+        total = total_b[:ROWS] if t == 0 else total_a[ROWS * (t - 1) : ROWS * t]
+        stepped[:, lanes] = weight[:, lanes] - learn_rate * (total * rate)
     stepped_norm[...] = norm_weight[...] - learn_rate * (total_b[B_ROWS - 8 :] * rate)
     for t in range(COLS):
         new = stepped[:, LANES * t : LANES * t + LANES].astype(bf16)
@@ -256,34 +243,34 @@
     )(*far(pq, pk, pv, pm))
     got_a = shift(send_a, 0, 0, 1)
     heads, tails = jnp.concatenate([mq, mk], 1), jnp.concatenate([mv, mm.T], 1)
-    mine, theirs = jnp.where(even, heads, tails), shift(jnp.where(even, tails, heads), 0, 0, 1)
+    mine, theirs = jnp.where(even, heads, tails), jnp.where(even, tails, heads)
+    theirs, other = shift(theirs, 0, 0, 1), shift(mn, 0, 0, 1)
     weight = jnp.where(even, jnp.concatenate([mine, theirs]), jnp.concatenate([theirs, mine]))
-    other = shift(mn, 0, 0, 1)
     norm_weight = jnp.where(even, jnp.concatenate([mn, other]), jnp.concatenate([other, mn]))
     norm_weight = jnp.pad(norm_weight[None], ((0, 7), (0, LANES - ROWS)))
 
     a_shape, b_shape = (NZ, A_ROWS, LANES), (NX, B_ROWS, LANES)
-    *b, extra = call(
+    b = call(
         split_b_kernel,
-        [FAR(b_shape, f32)] * NZ + [pltpu.VMEM((NZ, NX, ROWS - EXTRA, LANES), f32)],
+        [FAR(b_shape, f32)] * NZ,
         hbm(2) + vmem(2),
         [pltpu.VMEM((SPLIT, 1280), f32), pltpu.VMEM((NZ, *b_shape), f32), dma((2, chunks_b)), dma((NZ,))],
-        hbm(NZ) + vmem(1),
+        hbm(NZ),
     )(*far(pq, pv), *near(got_b, norm))
     got = [b[0]]
-    for steps in ((3, 5), (2, 6, 4, 1, 7)):
+    for steps in ((2, 6), (3, 5, 4, 1, 7)):
         got += [shift(b[r], r, 0) for r in steps]
     b = got
     a = call(
         split_a_kernel,
         [FAR(a_shape, f32)] + [pltpu.VMEM(a_shape, f32)] * 3,
-        hbm(4) + vmem(2),
+        hbm(4) + vmem(1),
         [
             pltpu.VMEM((640 - SPLIT, 1280), f32),
             pltpu.VMEM((4, NX, ROWS, LANES), f32),
             dma((2, chunks_a)),
         ],
-    )(*far(pq, pk, pv, pm), *near(got_a, extra))
+    )(*far(pq, pk, pv, pm), *near(got_a))
     a = shift_x(a)
     a, b, weight, norm_weight = lax.optimization_barrier((a, b, weight, norm_weight))
     a = call(

time: 130 us -> 122 us (0.938)
  waiting for transfers between devices: 47.2 us -> 31.1 us
  starting transfers between devices: 59.5 us -> 69.4 us
  Pallas kernels: 19.6 us -> 17.7 us
    ppermute x26, starting transfers between devices: 51.2 us -> 62.3 us  [shift(): return lax.ppermute(v, CHIPS, pairs)]
    ppermute x26, waiting for transfers between devices: 28 us -> 17.5 us  [shift(): return lax.ppermute(v, CHIPS, pairs)]
    all_to_all x2, waiting for transfers between devices: 19.2 us -> 13.6 us  [spread(): return lax.all_to_all(v, 'z', 0, 0, tiled=True)]
    pallas_call x1, Pallas kernels: 2.51 us -> 1.18 us  [on_device(): call(pick_kernel, pltpu.VMEM((SPLIT, 1280), f32), hbm(2), [dma((chunks_b,...]
  transfers between devices with their start and end apart: 28 -> 28, of which waited for: 13 -> 14; matrix products, arithmetic and copies ran while one was open for 2% -> 2% of each run, Pallas kernels for 9% -> 9%
where the time goes in v1:
time: 122 us
  starting transfers between devices  69.4 us (57%)
  waiting for transfers between devices  31.1 us (25%)
  Pallas kernels  17.7 us (15%)
  local copies, waits for them, and re-layouts  2.2 us (2%)
    ppermute x26, starting transfers between devices, shift(): return lax.ppermute(v, CHIPS, pairs)  62.3 us
    ppermute x26, waiting for transfers between devices, shift(): return lax.ppermute(v, CHIPS, pairs)  17.5 us
    all_to_all x2, waiting for transfers between devices, spread(): return lax.all_to_all(v, 'z', 0, 0, tiled=True)  13.6 us
    all_to_all x2, starting transfers between devices, spread(): return lax.all_to_all(v, 'z', 0, 0, tiled=True)  7.09 us
    pallas_call x1, Pallas kernels, on_device(): call(split_a_kernel, [FAR(a_shape, f32)] + [pltpu.VMEM(a_shape, f32)] * 3...  4.43 us
  transfers between devices with their start and end apart: 28, of which 14 were waited for; matrix products, arithmetic and copies ran while one was open for 2% of the time, Pallas kernels for 9%

profile of v1, /device:TPU:1, one launch (start us, length us, event | category | flops | bytes accessed | tf_op | source)
XLA Modules:
  0.0 121.9 jit_solution(12445331013971108076)
XLA Ops:
  0.6 1.9 %shard_map.177 = f32[512,1280]{1,0:T(8,128)S(1)} custom-call(f32[320,1280]{1,0:T(8,128)} %bitcast.32, f32[320,1280]{1,0:T(8,128)} %bitcast.40, f32[320,1280]{1,0:T(8,128)} %bitcast.36, f32[320,1280]{1,0:T(8,128)} %bitcast.42), custom_call_target="tpu_custom_call" | custom-call | tf_op jit(solution)/shard_map/pallas_call | solution.py:241
  2.6 3.3 %collective-permute-start = (f32[512,1280]{1,0:T(8,128)S(1)}, f32[512,1280]{1,0:T(8,128)S(1)}, u32[]{:S(2)}, u32[]{:S(2)}) collective-permute-start(f32[512,1280]{1,0:T(8,128)S(1)} %shard_map.177), channel_id=1, source_target_pairs={{0,4},{4,0},{8,12},{12,8},{16,20},{20,16},{24,28},{28,24},{32,36},... | collective-permute-start | bytes 7864328 | tf_op jit(solution)/shard_map/ppermute | solution.py:29
  7.2 3.2 %collective-permute-done.got = f32[512,1280]{1,0:T(8,128)S(1)} collective-permute-done((f32[512,1280]{1,0:T(8,128)S(1)}, f32[512,1280]{1,0:T(8,128)S(1)}, u32[]{:S(2)}, u32[]{:S(2)}) %collective-permute-start) | collective-permute-done | bytes 2621472 | tf_op jit(solution)/shard_map/ppermute | solution.py:29
  10.4 4.4 %shard_map.178 = (f32[8,160,128]{2,1,0:T(8,128)}, f32[8,160,128]{2,1,0:T(8,128)}, f32[8,160,128]{2,1,0:T(8,128)}, f32[8,160,128]{2,1,0:T(8,128)}) custom-call(f32[320,1280]{1,0:T(8,128)} %bitcast.34, f32[320,1280]{1,0:T(8,128)} %bitcast.41, f32[320,1280]{1,0:T(8,128)} %bitcast.38, f32[320,1280]{1,0:T(8,128)} %bitcast.43, ...), custom_call_target="tpu_custom_call" | custom-call | tf_op jit(solution)/shard_map/pallas_call | solution.py:264
  14.9 2.0 %collective-permute-start.2 = (f32[8,160,128]{2,1,0:T(8,128)}, f32[8,160,128]{2,1,0:T(8,128)S(1)}, u32[]{:S(2)}, u32[]{:S(2)}) collective-permute-start(f32[8,160,128]{2,1,0:T(8,128)} %get-tuple-element.59), channel_id=1, source_target_pairs={{0,16},{4,20},{8,24},{12,28},{16,0},{20,4},{24,8},{28,12},{32,48},... | collective-permute-start | bytes 1966088 | tf_op jit(solution)/shard_map/ppermute | solution.py:29
  18.0 1.2 collective-permute-start.5
  20.6 2.4 %shard_map.180 = (f32[4,48,128]{2,1,0:T(8,128)}, f32[4,48,128]{2,1,0:T(8,128)}, f32[4,48,128]{2,1,0:T(8,128)}, f32[4,48,128]{2,1,0:T(8,128)}, f32[4,48,128]{2,1,...) custom-call(f32[320,1280]{1,0:T(8,128)} %bitcast.35, f32[320,1280]{1,0:T(8,128)} %bitcast.39, ...), custom_call_target="tpu_custom_call" | custom-call | tf_op jit(solution)/shard_map/pallas_call | solution.py:253
  23.1 3.1 %collective-permute-start.6 = (f32[4,48,128]{2,1,0:T(8,128)}, f32[4,48,128]{2,1,0:T(8,128)S(1)}, u32[]{:S(2)}, u32[]{:S(2)}) collective-permute-start(f32[4,48,128]{2,1,0:T(8,128)} %get-tuple-element.62), channel_id=1, source_target_pairs={{0,64},{4,68},{8,72},{12,76},{16,80},{20,84},{24,88},{28,92},{32,9... | collective-permute-start | bytes 294920 | tf_op jit(solution)/shard_map/ppermute | solution.py:29
  27.7 3.0 %collective-permute-start.7 = (f32[4,48,128]{2,1,0:T(8,128)}, f32[4,48,128]{2,1,0:T(8,128)S(1)}, u32[]{:S(2)}, u32[]{:S(2)}) collective-permute-start(f32[4,48,128]{2,1,0:T(8,128)} %get-tuple-element.63), channel_id=1, source_target_pairs={{0,192},{4,196},{8,200},{12,204},{16,208},{20,212},{24,216},{28,22... | collective-permute-start | bytes 294920 | tf_op jit(solution)/shard_map/ppermute | solution.py:29
  30.6 2.3 %collective-permute-done.6.refs_1_ = f32[4,48,128]{2,1,0:T(8,128)S(1)} collective-permute-done((f32[4,48,128]{2,1,0:T(8,128)}, f32[4,48,128]{2,1,0:T(8,128)S(1)}, u32[]{:S(2)}, u32[]{:S(2)}) %collective-permute-start.6) | collective-permute-done | bytes 98336 | tf_op jit(solution)/shard_map/ppermute | solution.py:29
  33.0 2.1 %collective-permute-start.8 = (f32[4,48,128]{2,1,0:T(8,128)}, f32[4,48,128]{2,1,0:T(8,128)S(1)}, u32[]{:S(2)}, u32[]{:S(2)}) collective-permute-start(f32[4,48,128]{2,1,0:T(8,128)} %get-tuple-element.64), channel_id=1, source_target_pairs={{0,96},{4,100},{8,104},{12,108},{16,112},{20,116},{24,120},{28,124... | collective-permute-start | bytes 294920 | tf_op jit(solution)/shard_map/ppermute | solution.py:29
  35.0 2.0 %collective-permute-done.7.refs_2_ = f32[4,48,128]{2,1,0:T(8,128)S(1)} collective-permute-done((f32[4,48,128]{2,1,0:T(8,128)}, f32[4,48,128]{2,1,0:T(8,128)S(1)}, u32[]{:S(2)}, u32[]{:S(2)}) %collective-permute-start.7) | collective-permute-done | bytes 98336 | tf_op jit(solution)/shard_map/ppermute | solution.py:29
  37.0 1.7 %collective-permute-start.9 = (f32[4,48,128]{2,1,0:T(8,128)}, f32[4,48,128]{2,1,0:T(8,128)S(1)}, u32[]{:S(2)}, u32[]{:S(2)}) collective-permute-start(f32[4,48,128]{2,1,0:T(8,128)} %get-tuple-element.65), channel_id=1, source_target_pairs={{0,160},{4,164},{8,168},{12,172},{16,176},{20,180},{24,184},{28,18... | collective-permute-start | bytes 294920 | tf_op jit(solution)/shard_map/ppermute | solution.py:29
  39.8 6.4 %collective-permute-start.10 = (f32[4,48,128]{2,1,0:T(8,128)}, f32[4,48,128]{2,1,0:T(8,128)S(1)}, u32[]{:S(2)}, u32[]{:S(2)}) collective-permute-start(f32[4,48,128]{2,1,0:T(8,128)} %get-tuple-element.66), channel_id=1, source_target_pairs={{0,128},{4,132},{8,136},{12,140},{16,144},{20,148},{24,152},{28,15... | collective-permute-start | bytes 294920 | tf_op jit(solution)/shard_map/ppermute | solution.py:29
  46.2 2.7 %collective-permute-start.11 = (f32[4,48,128]{2,1,0:T(8,128)}, f32[4,48,128]{2,1,0:T(8,128)S(1)}, u32[]{:S(2)}, u32[]{:S(2)}) collective-permute-start(f32[4,48,128]{2,1,0:T(8,128)} %get-tuple-element.67), channel_id=1, source_target_pairs={{0,32},{4,36},{8,40},{12,44},{16,48},{20,52},{24,56},{28,60},{32,6... | collective-permute-start | bytes 294920 | tf_op jit(solution)/shard_map/ppermute | solution.py:29
  49.1 3.5 %collective-permute-start.12 = (f32[4,48,128]{2,1,0:T(8,128)}, f32[4,48,128]{2,1,0:T(8,128)S(1)}, u32[]{:S(2)}, u32[]{:S(2)}) collective-permute-start(f32[4,48,128]{2,1,0:T(8,128)} %get-tuple-element.68), channel_id=1, source_target_pairs={{0,224},{4,228},{8,232},{12,236},{16,240},{20,244},{24,248},{28,25... | collective-permute-start | bytes 294920 | tf_op jit(solution)/shard_map/ppermute | solution.py:29
  52.6 1.5 %collective-permute-done.11.refs_6_ = f32[4,48,128]{2,1,0:T(8,128)S(1)} collective-permute-done((f32[4,48,128]{2,1,0:T(8,128)}, f32[4,48,128]{2,1,0:T(8,128)S(1)}, u32[]{:S(2)}, u32[]{:S(2)}) %collective-permute-start.11) | collective-permute-done | bytes 98336 | tf_op jit(solution)/shard_map/ppermute | solution.py:29
  54.1 3.7 %collective-permute-done.12.refs_7_ = f32[4,48,128]{2,1,0:T(8,128)S(1)} collective-permute-done((f32[4,48,128]{2,1,0:T(8,128)}, f32[4,48,128]{2,1,0:T(8,128)S(1)}, u32[]{:S(2)}, u32[]{:S(2)}) %collective-permute-start.12) | collective-permute-done | bytes 98336 | tf_op jit(solution)/shard_map/ppermute | solution.py:29
  57.7 2.0 %shard_map.181 = f32[8,160,128]{2,1,0:T(8,128)} custom-call(f32[8,160,128]{2,1,0:T(8,128)} %get-tuple-element.69.a0, f32[8,160,128]{2,1,0:T(8,128)S(1)} %collective-permute-done.1.a1, f32[8,160,128]{2,1,0:T(8,128)S(1)} %collective-permute-done.2.a2, f32[8,160,128]{2,1,0:T(8,128)S(1)} %collective-permute-done.3.a3), custom_call_target="tpu_custom_call" | custom-call | tf_op jit(solution)/shard_map/pallas_call | solution.py:276
  59.8 3.6 %all-to-all-start = ((f32[8,160,128]{2,1,0:T(8,128)}), f32[8,160,128]{2,1,0:T(8,128)S(1)}, u32[]{:S(2)}, u32[]{:S(2)}) async-start(f32[8,160,128]{2,1,0:T(8,128)} %shard_map.181), calls=%async_computation | async-start | bytes 1310720 | tf_op jit(solution)/shard_map/all_to_all | solution.py:38
  65.4 1.9 %collective-permute-start.17 = (f32[48,128]{1,0:T(8,128)S(1)}, f32[48,128]{1,0:T(8,128)S(1)}, u32[]{:S(2)}, u32[]{:S(2)}) collective-permute-start(f32[48,128]{1,0:T(8,128)S(1)} %get-tuple-element.84), channel_id=1, source_target_pairs={{0,24},{4,28},{8,0},{12,4},{16,8},{20,12},{24,16},{28,20},{32,56},... | collective-permute-start | bytes 73736 | tf_op jit(solution)/shard_map/ppermute | solution.py:29
  69.2 9.4 %all-to-all-done.a = f32[8,160,128]{2,1,0:T(8,128)S(1)} async-done(((f32[8,160,128]{2,1,0:T(8,128)}), f32[8,160,128]{2,1,0:T(8,128)S(1)}, u32[]{:S(2)}, u32[]{:S(2)}) %all-to-all-start) | async-done | bytes 655392 | tf_op jit(solution)/shard_map/all_to_all | solution.py:38
  79.4 3.5 %all-to-all-start.1 = ((bf16[8,208,128]{2,1,0:T(8,128)(2,1)}), bf16[8,208,128]{2,1,0:T(8,128)(2,1)S(1)}, u32[]{:S(2)}, u32[]{:S(2)}) async-start(bf16[8,208,128]{2,1,0:T(8,128)(2,1)} %get-tuple-element.87), calls=%async_computation.1 | async-start | bytes 851968 | tf_op jit(solution)/shard_map/all_to_all | solution.py:38
  82.9 6.2 %collective-permute-start.24 = (f32[20,640]{1,0:T(8,128)S(1)}, f32[20,640]{1,0:T(8,128)S(1)}, u32[]{:S(2)}, u32[]{:S(2)}) collective-permute-start(f32[20,640]{1,0:T(8,128)S(1)} %constant_dynamic-slice_fusion.1), channel_id=1, source_target_pairs={{0,4},{4,0},{8,12},{12,8},{16,20},{20,16},{24,28},{28,24},{32,36},... | collective-permute-start | bytes 153608 | tf_op jit(solution)/shard_map/ppermute | solution.py:29
  89.7 4.2 %all-to-all-done.1.a0 = bf16[8,208,128]{2,1,0:T(8,128)(2,1)S(1)} async-done(((bf16[8,208,128]{2,1,0:T(8,128)(2,1)}), bf16[8,208,128]{2,1,0:T(8,128)(2,1)S(1)}, u32[]{:S(2)}, u32[]{:S(2)}) %all-to-all-start.1) | async-done | bytes 426016 | tf_op jit(solution)/shard_map/all_to_all | solution.py:38
  94.0 2.1 %collective-permute-start.21 = (bf16[8,208,128]{2,1,0:T(8,128)(2,1)S(1)}, bf16[8,208,128]{2,1,0:T(8,128)(2,1)S(1)}, u32[]{:S(2)}, u32[]{:S(2)}) collective-permute-start(bf16[8,208,128]{2,1,0:T(8,128)(2,1)S(1)} %all-to-all-done.1.a0), channel_id=1, source_target_pairs={{0,16},{4,20},{8,24},{12,28},{16,0},{20,4},{24,8},{28,12},{32,48},... | collective-permute-start | bytes 1277960 | tf_op jit(solution)/shard_map/ppermute | solution.py:29
  96.9 7.7 %collective-permute-start.18 = (bf16[8,208,128]{2,1,0:T(8,128)(2,1)S(1)}, bf16[8,208,128]{2,1,0:T(8,128)(2,1)S(1)}, u32[]{:S(2)}, u32[]{:S(2)}) collective-permute-start(bf16[8,208,128]{2,1,0:T(8,128)(2,1)S(1)} %all-to-all-done.1.a0), channel_id=1, source_target_pairs={{0,4},{4,0},{8,12},{12,8},{16,20},{20,16},{24,28},{28,24},{32,36},... | collective-permute-start | bytes 1277960 | tf_op jit(solution)/shard_map/ppermute | solution.py:29
  104.6 6.2 %collective-permute-start.25 = (bf16[8,208,128]{2,1,0:T(8,128)(2,1)S(1)}, bf16[8,208,128]{2,1,0:T(8,128)(2,1)S(1)}, u32[]{:S(2)}, u32[]{:S(2)}) collective-permute-start(bf16[8,208,128]{2,1,0:T(8,128)(2,1)S(1)} %collective-permute-done.23.a3), channel_id=1, source_target_pairs={{0,4},{4,0},{8,12},{12,8},{16,20},{20,16},{24,28},{28,24},{32,36},... | collective-permute-start | bytes 1277960 | tf_op jit(solution)/shard_map/ppermute | solution.py:29
  110.8 1.6 %collective-permute-start.22 = (bf16[8,208,128]{2,1,0:T(8,128)(2,1)S(1)}, bf16[8,208,128]{2,1,0:T(8,128)(2,1)S(1)}, u32[]{:S(2)}, u32[]{:S(2)}) collective-permute-start(bf16[8,208,128]{2,1,0:T(8,128)(2,1)S(1)} %collective-permute-done.21.a2), channel_id=1, source_target_pairs={{0,4},{4,0},{8,12},{12,8},{16,20},{20,16},{24,28},{28,24},{32,36},... | collective-permute-start | bytes 1277960 | tf_op jit(solution)/shard_map/ppermute | solution.py:29
  112.4 4.4 %collective-permute-start.20 = (bf16[8,208,128]{2,1,0:T(8,128)(2,1)S(1)}, bf16[8,208,128]{2,1,0:T(8,128)(2,1)S(1)}, u32[]{:S(2)}, u32[]{:S(2)}) collective-permute-start(bf16[8,208,128]{2,1,0:T(8,128)(2,1)S(1)} %collective-permute-done.19.a1), channel_id=1, source_target_pairs={{0,4},{4,0},{8,12},{12,8},{16,20},{20,16},{24,28},{28,24},{32,36},... | collective-permute-start | bytes 1277960 | tf_op jit(solution)/shard_map/ppermute | solution.py:29
  117.8 2.0 %shard_map.184 = (bf16[320,1280]{1,0:T(8,128)(2,1)}, bf16[320,1280]{1,0:T(8,128)(2,1)}, bf16[320,1280]{1,0:T(8,128)(2,1)}, bf16[320,1280]{1,0:T(8,128)(2,1)}) custom-call(bf16[8,208,128]{2,1,0:T(8,128)(2,1)S(1)} %all-to-all-done.1.a0, bf16[8,208,128]{2,1,0:T(8,128)(2,1)S(1)} %collective-permute-done.19.a1, ...), custom_call_target="tpu_custom_call" | custom-call | tf_op jit(solution)/shard_map/pallas_call | solution.py:312
  119.8 2.0 %shard_map.185 = (bf16[320,1280]{1,0:T(8,128)(2,1)}, bf16[320,1280]{1,0:T(8,128)(2,1)}, bf16[320,1280]{1,0:T(8,128)(2,1)}, bf16[320,1280]{1,0:T(8,128)(2,1)}) custom-call(bf16[8,208,128]{2,1,0:T(8,128)(2,1)S(1)} %collective-permute-done.18.a0, ...), custom_call_target="tpu_custom_call", output_to_operand_aliasing={{0}: (4, {}), {1}: (5, {}), {2}: (6, {}), {3}: (7, {})} | custom-call | tf_op jit(solution)/shard_map/pallas_call | solution.py:314
  (69 shorter events, 13.5 us)
Async XLA Ops:
  2.6 7.8 %collective-permute-start = (f32[512,1280]{1,0:T(8,128)S(1)}, f32[512,1280]{1,0:T(8,128)S(1)}, u32[]{:S(2)}, u32[]{:S(2)}) collective-permute-start(f32[512,1280]{1,0:T(8,128)S(1)} %shard_map.177), channel_id=1, source_target_pairs={{0,4},{4,0},{8,12},{12,8},{16,20},{20,16},{24,28},{28,24},{32,36},... | collective-permute-start | bytes 7864328 | tf_op jit(solution)/shard_map/ppermute | solution.py:29
  7.1 11.0 %copy-start.4 = (f32[1,1280]{1,0:T(1,128)S(1)}, f32[1,1280]{1,0:T(1,128)}, u32[]{:S(2)}) copy-start(f32[1,1280]{1,0:T(1,128)} %param.14) | copy-start | bytes 15364
  7.1 13.0 %copy-start.5 = (f32[20]{0:T(128)S(1)}, f32[20]{0:T(128)}, u32[]{:S(2)}) copy-start(f32[20]{0:T(128)} %param.19) | copy-start | bytes 244
  7.1 13.5 %collective-permute-start.4 = (f32[128,1280]{1,0:T(8,128)S(1)}, f32[128,1280]{1,0:T(8,128)S(1)}, u32[]{:S(2)}, u32[]{:S(2)}) collective-permute-start(f32[128,1280]{1,0:T(8,128)S(1)} %shard_map.179), channel_id=1, source_target_pairs={{0,4},{4,0},{8,12},{12,8},{16,20},{20,16},{24,28},{28,24},{32,36},... | collective-permute-start | bytes 1966088 | tf_op jit(solution)/shard_map/ppermute | solution.py:29
  14.8 42.9 %collective-permute-start.1 = (f32[8,160,128]{2,1,0:T(8,128)}, f32[8,160,128]{2,1,0:T(8,128)S(1)}, u32[]{:S(2)}, u32[]{:S(2)}) collective-permute-start(f32[8,160,128]{2,1,0:T(8,128)} %get-tuple-element.58), channel_id=1, source_target_pairs={{0,8},{4,12},{8,16},{12,20},{16,24},{20,28},{24,0},{28,4},{32,40},... | collective-permute-start | bytes 1966088 | tf_op jit(solution)/shard_map/ppermute | solution.py:29
  14.9 42.8 %collective-permute-start.2 = (f32[8,160,128]{2,1,0:T(8,128)}, f32[8,160,128]{2,1,0:T(8,128)S(1)}, u32[]{:S(2)}, u32[]{:S(2)}) collective-permute-start(f32[8,160,128]{2,1,0:T(8,128)} %get-tuple-element.59), channel_id=1, source_target_pairs={{0,16},{4,20},{8,24},{12,28},{16,0},{20,4},{24,8},{28,12},{32,48},... | collective-permute-start | bytes 1966088 | tf_op jit(solution)/shard_map/ppermute | solution.py:29
  16.9 40.8 %collective-permute-start.3 = (f32[8,160,128]{2,1,0:T(8,128)}, f32[8,160,128]{2,1,0:T(8,128)S(1)}, u32[]{:S(2)}, u32[]{:S(2)}) collective-permute-start(f32[8,160,128]{2,1,0:T(8,128)} %get-tuple-element.60), channel_id=1, source_target_pairs={{0,24},{4,28},{8,0},{12,4},{16,8},{20,12},{24,16},{28,20},{32,56},... | collective-permute-start | bytes 1966088 | tf_op jit(solution)/shard_map/ppermute | solution.py:29
  18.0 2.0 %collective-permute-start.5 = (f32[1,1280]{1,0:T(1,128)S(1)}, f32[1,1280]{1,0:T(1,128)S(1)}, u32[]{:S(2)}, u32[]{:S(2)}) collective-permute-start(f32[1,1280]{1,0:T(1,128)S(1)} %copy-done.4), channel_id=1, source_target_pairs={{0,4},{4,0},{8,12},{12,8},{16,20},{20,16},{24,28},{28,24},{32,36},... | collective-permute-start | bytes 15368 | tf_op jit(solution)/shard_map/ppermute | solution.py:29
  20.1 6.2 %collective-permute-start.14 = (f32[20]{0:T(128)S(1)}, f32[20]{0:T(128)S(1)}, u32[]{:S(2)}, u32[]{:S(2)}) collective-permute-start(f32[20]{0:T(128)S(1)} %copy-done.5), channel_id=1, source_target_pairs={{0,4},{4,0},{8,12},{12,8},{16,20},{20,16},{24,28},{28,24},{32,36},... | collective-permute-start | bytes 248 | tf_op jit(solution)/shard_map/ppermute | solution.py:29
  20.6 5.6 %copy-start = (f32[320,20]{0,1:T(8,128)S(1)}, f32[320,20]{0,1:T(8,128)}, u32[]{:S(2)}) copy-start(f32[320,20]{0,1:T(8,128)} %param.18) | copy-start | bytes 76804
  20.6 5.5 %copy-start.1 = (f32[20,320]{1,0:T(8,128)S(1)}, f32[20,320]{1,0:T(8,128)}, u32[]{:S(2)}) copy-start(f32[20,320]{1,0:T(8,128)} %param.17) | copy-start | bytes 76804
  23.1 9.9 %collective-permute-start.6 = (f32[4,48,128]{2,1,0:T(8,128)}, f32[4,48,128]{2,1,0:T(8,128)S(1)}, u32[]{:S(2)}, u32[]{:S(2)}) collective-permute-start(f32[4,48,128]{2,1,0:T(8,128)} %get-tuple-element.62), channel_id=1, source_target_pairs={{0,64},{4,68},{8,72},{12,76},{16,80},{20,84},{24,88},{28,92},{32,9... | collective-permute-start | bytes 294920 | tf_op jit(solution)/shard_map/ppermute | solution.py:29
  26.2 1.4 %collective-permute-start.13 = (f32[20,640]{1,0:T(8,128)S(1)}, f32[20,640]{1,0:T(8,128)S(1)}, u32[]{:S(2)}, u32[]{:S(2)}) collective-permute-start(f32[20,640]{1,0:T(8,128)S(1)} %get-tuple-element.107), channel_id=1, source_target_pairs={{0,4},{4,0},{8,12},{12,8},{16,20},{20,16},{24,28},{28,24},{32,36},... | collective-permute-start | bytes 153608 | tf_op jit(solution)/shard_map/ppermute | solution.py:29
  27.7 9.4 %collective-permute-start.7 = (f32[4,48,128]{2,1,0:T(8,128)}, f32[4,48,128]{2,1,0:T(8,128)S(1)}, u32[]{:S(2)}, u32[]{:S(2)}) collective-permute-start(f32[4,48,128]{2,1,0:T(8,128)} %get-tuple-element.63), channel_id=1, source_target_pairs={{0,192},{4,196},{8,200},{12,204},{16,208},{20,212},{24,216},{28,22... | collective-permute-start | bytes 294920 | tf_op jit(solution)/shard_map/ppermute | solution.py:29
  33.0 6.8 %collective-permute-start.8 = (f32[4,48,128]{2,1,0:T(8,128)}, f32[4,48,128]{2,1,0:T(8,128)S(1)}, u32[]{:S(2)}, u32[]{:S(2)}) collective-permute-start(f32[4,48,128]{2,1,0:T(8,128)} %get-tuple-element.64), channel_id=1, source_target_pairs={{0,96},{4,100},{8,104},{12,108},{16,112},{20,116},{24,120},{28,124... | collective-permute-start | bytes 294920 | tf_op jit(solution)/shard_map/ppermute | solution.py:29
  37.0 9.2 %collective-permute-start.9 = (f32[4,48,128]{2,1,0:T(8,128)}, f32[4,48,128]{2,1,0:T(8,128)S(1)}, u32[]{:S(2)}, u32[]{:S(2)}) collective-permute-start(f32[4,48,128]{2,1,0:T(8,128)} %get-tuple-element.65), channel_id=1, source_target_pairs={{0,160},{4,164},{8,168},{12,172},{16,176},{20,180},{24,184},{28,18... | collective-permute-start | bytes 294920 | tf_op jit(solution)/shard_map/ppermute | solution.py:29
  39.8 9.4 %collective-permute-start.10 = (f32[4,48,128]{2,1,0:T(8,128)}, f32[4,48,128]{2,1,0:T(8,128)S(1)}, u32[]{:S(2)}, u32[]{:S(2)}) collective-permute-start(f32[4,48,128]{2,1,0:T(8,128)} %get-tuple-element.66), channel_id=1, source_target_pairs={{0,128},{4,132},{8,136},{12,140},{16,144},{20,148},{24,152},{28,15... | collective-permute-start | bytes 294920 | tf_op jit(solution)/shard_map/ppermute | solution.py:29
  46.2 7.8 %collective-permute-start.11 = (f32[4,48,128]{2,1,0:T(8,128)}, f32[4,48,128]{2,1,0:T(8,128)S(1)}, u32[]{:S(2)}, u32[]{:S(2)}) collective-permute-start(f32[4,48,128]{2,1,0:T(8,128)} %get-tuple-element.67), channel_id=1, source_target_pairs={{0,32},{4,36},{8,40},{12,44},{16,48},{20,52},{24,56},{28,60},{32,6... | collective-permute-start | bytes 294920 | tf_op jit(solution)/shard_map/ppermute | solution.py:29
  49.1 8.6 %collective-permute-start.12 = (f32[4,48,128]{2,1,0:T(8,128)}, f32[4,48,128]{2,1,0:T(8,128)S(1)}, u32[]{:S(2)}, u32[]{:S(2)}) collective-permute-start(f32[4,48,128]{2,1,0:T(8,128)} %get-tuple-element.68), channel_id=1, source_target_pairs={{0,224},{4,228},{8,232},{12,236},{16,240},{20,244},{24,248},{28,25... | collective-permute-start | bytes 294920 | tf_op jit(solution)/shard_map/ppermute | solution.py:29
  59.8 18.8 %all-to-all-start = ((f32[8,160,128]{2,1,0:T(8,128)}), f32[8,160,128]{2,1,0:T(8,128)S(1)}, u32[]{:S(2)}, u32[]{:S(2)}) async-start(f32[8,160,128]{2,1,0:T(8,128)} %shard_map.181), calls=%async_computation | async-start | bytes 1310720 | tf_op jit(solution)/shard_map/all_to_all | solution.py:38
  64.4 4.0 %collective-permute-start.15 = (f32[48,128]{1,0:T(8,128)S(1)}, f32[48,128]{1,0:T(8,128)S(1)}, u32[]{:S(2)}, u32[]{:S(2)}) collective-permute-start(f32[48,128]{1,0:T(8,128)S(1)} %get-tuple-element.82), channel_id=1, source_target_pairs={{0,8},{4,12},{8,16},{12,20},{16,24},{20,28},{24,0},{28,4},{32,40},... | collective-permute-start | bytes 73736 | tf_op jit(solution)/shard_map/ppermute | solution.py:29
  64.8 4.2 %collective-permute-start.16 = (f32[48,128]{1,0:T(8,128)S(1)}, f32[48,128]{1,0:T(8,128)S(1)}, u32[]{:S(2)}, u32[]{:S(2)}) collective-permute-start(f32[48,128]{1,0:T(8,128)S(1)} %get-tuple-element.83), channel_id=1, source_target_pairs={{0,16},{4,20},{8,24},{12,28},{16,0},{20,4},{24,8},{28,12},{32,48},... | collective-permute-start | bytes 73736 | tf_op jit(solution)/shard_map/ppermute | solution.py:29
  65.4 3.8 %collective-permute-start.17 = (f32[48,128]{1,0:T(8,128)S(1)}, f32[48,128]{1,0:T(8,128)S(1)}, u32[]{:S(2)}, u32[]{:S(2)}) collective-permute-start(f32[48,128]{1,0:T(8,128)S(1)} %get-tuple-element.84), channel_id=1, source_target_pairs={{0,24},{4,28},{8,0},{12,4},{16,8},{20,12},{24,16},{28,20},{32,56},... | collective-permute-start | bytes 73736 | tf_op jit(solution)/shard_map/ppermute | solution.py:29
  79.4 14.6 %all-to-all-start.1 = ((bf16[8,208,128]{2,1,0:T(8,128)(2,1)}), bf16[8,208,128]{2,1,0:T(8,128)(2,1)S(1)}, u32[]{:S(2)}, u32[]{:S(2)}) async-start(bf16[8,208,128]{2,1,0:T(8,128)(2,1)} %get-tuple-element.87), calls=%async_computation.1 | async-start | bytes 851968 | tf_op jit(solution)/shard_map/all_to_all | solution.py:38
  82.9 13.2 %collective-permute-start.24 = (f32[20,640]{1,0:T(8,128)S(1)}, f32[20,640]{1,0:T(8,128)S(1)}, u32[]{:S(2)}, u32[]{:S(2)}) collective-permute-start(f32[20,640]{1,0:T(8,128)S(1)} %constant_dynamic-slice_fusion.1), channel_id=1, source_target_pairs={{0,4},{4,0},{8,12},{12,8},{16,20},{20,16},{24,28},{28,24},{32,36},... | collective-permute-start | bytes 153608 | tf_op jit(solution)/shard_map/ppermute | solution.py:29
  94.0 10.6 %collective-permute-start.23 = (bf16[8,208,128]{2,1,0:T(8,128)(2,1)S(1)}, bf16[8,208,128]{2,1,0:T(8,128)(2,1)S(1)}, u32[]{:S(2)}, u32[]{:S(2)}) collective-permute-start(bf16[8,208,128]{2,1,0:T(8,128)(2,1)S(1)} %all-to-all-done.1.a0), channel_id=1, source_target_pairs={{0,24},{4,28},{8,0},{12,4},{16,8},{20,12},{24,16},{28,20},{32,56},... | collective-permute-start | bytes 1277960 | tf_op jit(solution)/shard_map/ppermute | solution.py:29
  94.0 16.8 %collective-permute-start.21 = (bf16[8,208,128]{2,1,0:T(8,128)(2,1)S(1)}, bf16[8,208,128]{2,1,0:T(8,128)(2,1)S(1)}, u32[]{:S(2)}, u32[]{:S(2)}) collective-permute-start(bf16[8,208,128]{2,1,0:T(8,128)(2,1)S(1)} %all-to-all-done.1.a0), channel_id=1, source_target_pairs={{0,16},{4,20},{8,24},{12,28},{16,0},{20,4},{24,8},{28,12},{32,48},... | collective-permute-start | bytes 1277960 | tf_op jit(solution)/shard_map/ppermute | solution.py:29
  96.1 16.3 %collective-permute-start.19 = (bf16[8,208,128]{2,1,0:T(8,128)(2,1)S(1)}, bf16[8,208,128]{2,1,0:T(8,128)(2,1)S(1)}, u32[]{:S(2)}, u32[]{:S(2)}) collective-permute-start(bf16[8,208,128]{2,1,0:T(8,128)(2,1)S(1)} %all-to-all-done.1.a0), channel_id=1, source_target_pairs={{0,8},{4,12},{8,16},{12,20},{16,24},{20,28},{24,0},{28,4},{32,40},... | collective-permute-start | bytes 1277960 | tf_op jit(solution)/shard_map/ppermute | solution.py:29
  96.9 22.9 %collective-permute-start.18 = (bf16[8,208,128]{2,1,0:T(8,128)(2,1)S(1)}, bf16[8,208,128]{2,1,0:T(8,128)(2,1)S(1)}, u32[]{:S(2)}, u32[]{:S(2)}) collective-permute-start(bf16[8,208,128]{2,1,0:T(8,128)(2,1)S(1)} %all-to-all-done.1.a0), channel_id=1, source_target_pairs={{0,4},{4,0},{8,12},{12,8},{16,20},{20,16},{24,28},{28,24},{32,36},... | collective-permute-start | bytes 1277960 | tf_op jit(solution)/shard_map/ppermute | solution.py:29
  104.6 15.1 %collective-permute-start.25 = (bf16[8,208,128]{2,1,0:T(8,128)(2,1)S(1)}, bf16[8,208,128]{2,1,0:T(8,128)(2,1)S(1)}, u32[]{:S(2)}, u32[]{:S(2)}) collective-permute-start(bf16[8,208,128]{2,1,0:T(8,128)(2,1)S(1)} %collective-permute-done.23.a3), channel_id=1, source_target_pairs={{0,4},{4,0},{8,12},{12,8},{16,20},{20,16},{24,28},{28,24},{32,36},... | collective-permute-start | bytes 1277960 | tf_op jit(solution)/shard_map/ppermute | solution.py:29
  110.8 8.9 %collective-permute-start.22 = (bf16[8,208,128]{2,1,0:T(8,128)(2,1)S(1)}, bf16[8,208,128]{2,1,0:T(8,128)(2,1)S(1)}, u32[]{:S(2)}, u32[]{:S(2)}) collective-permute-start(bf16[8,208,128]{2,1,0:T(8,128)(2,1)S(1)} %collective-permute-done.21.a2), channel_id=1, source_target_pairs={{0,4},{4,0},{8,12},{12,8},{16,20},{20,16},{24,28},{28,24},{32,36},... | collective-permute-start | bytes 1277960 | tf_op jit(solution)/shard_map/ppermute | solution.py:29
  112.4 7.3 %collective-permute-start.20 = (bf16[8,208,128]{2,1,0:T(8,128)(2,1)S(1)}, bf16[8,208,128]{2,1,0:T(8,128)(2,1)S(1)}, u32[]{:S(2)}, u32[]{:S(2)}) collective-permute-start(bf16[8,208,128]{2,1,0:T(8,128)(2,1)S(1)} %collective-permute-done.19.a1), channel_id=1, source_target_pairs={{0,4},{4,0},{8,12},{12,8},{16,20},{20,16},{24,28},{28,24},{32,36},... | collective-permute-start | bytes 1277960 | tf_op jit(solution)/shard_map/ppermute | solution.py:29
  (2 other events, 11.1 us)

commit v2 on v1

--- a/solution.py
+++ b/solution.py
@@ -30,8 +30,8 @@
 
 
 def shift_x(v):
-    far_one = shift(v[2], 0, 2)
-    return [v[0], shift(v[1], 0, 1), far_one, shift(v[3], 0, 3)]
+    near_ones = shift(v[1], 0, 1), shift(v[3], 0, 3)
+    return [v[0], near_ones[0], shift(v[2], 0, 2), near_ones[1]]
 
 
 def spread(v):
@@ -136,11 +136,13 @@
     return [pltpu.with_memory_space_constraint(v, pltpu.HBM) for v in arrays]
 
 
-def sum_a_kernel(a0, a1, a2, a3, out, own, sem):
-    copy = pltpu.make_async_copy(a0, own, sem)
-    copy.start()
-    copy.wait()
-    out[...] = own[...] + a1[...] + a2[...] + a3[...]
+def sum_a_kernel(a0, a1, a2, a3, out, own, sems):
+    copies = [pltpu.make_async_copy(a0.at[z], own.at[z], sems.at[z]) for z in range(NZ)]
+    for c in copies:
+        c.start()
+    for z, c in enumerate(copies):
+        c.wait()
+        out[z] = own[z] + a1[z] + a2[z] + a3[z]
 
 
 def sum_b_kernel(*refs):
@@ -169,12 +171,8 @@
         stepped[:, lanes] = weight[:, lanes] - learn_rate * (total * rate)
     stepped_norm[...] = norm_weight[...] - learn_rate * (total_b[B_ROWS - 8 :] * rate)
     for t in range(COLS):
-        new = stepped[:, LANES * t : LANES * t + LANES].astype(bf16)
-        for z in range(NZ):
-            out[z, ROWS * t : ROWS * t + ROWS] = new
-    new = stepped_norm[...].astype(bf16)
-    for z in range(NZ):
-        out[z, G_ROWS - 8 :] = new
+        out[ROWS * t : ROWS * t + ROWS] = stepped[:, LANES * t : LANES * t + LANES].astype(bf16)
+    out[G_ROWS - 8 :] = stepped_norm[...].astype(bf16)
 
 
 def turn_kernel(own, a0, a1, a2, a3, *refs):
@@ -189,17 +187,19 @@
             for j, out in enumerate(pair_out)
         ]
 
+    z0 = lax.axis_index("z")
+    for j, a in enumerate((a0, a1, a2, a3)):
+        for r in range(NZ):
+            chip = lax.rem(z0 + NZ - r, NZ) * NX + lax.rem(x + NX - j, NX)
+            rows = pl.ds(pl.multiple_of(chip * ROWS, 8), ROWS)
+            for t in range(COLS):
+                tile = a[r, ROWS * t : ROWS * t + ROWS, :]
+                turned[rows, LANES * t : LANES * t + LANES] = tile.astype(f32)
     for i in range(2):
-        for j, a in enumerate((a0, a1, a2, a3)):
-            place = lax.rem(x + NX - j, NX) * ROWS
-            for z in range(4):
-                rows = pl.ds(pl.multiple_of(place + z * NX * ROWS, 8), ROWS)
-                for t in range(COLS):
-                    tile = a[4 * i + z, ROWS * t : ROWS * t + ROWS, :]
-                    turned[rows, LANES * t : LANES * t + LANES] = tile.astype(f32)
+        half = slice(640 * i, 640 * i + 640)
         for t in range(COLS):
             lanes = slice(LANES * t, LANES * t + LANES)
-            pair[lanes, 640 * i : 640 * i + 640] = turned[:, lanes].T.astype(bf16)
+            pair[lanes, half] = turned[half, lanes].T.astype(bf16)
         for flip in range(2):
 
             @pl.when(core == (flip if own else 1 - flip))
@@ -258,7 +258,7 @@
         hbm(NZ),
     )(*far(pq, pv), *near(got_b, norm))
     got = [b[0]]
-    for steps in ((2, 6), (3, 5, 4, 1, 7)):
+    for steps in ((1, 7), (2, 6, 3, 5, 4)):
         got += [shift(b[r], r, 0) for r in steps]
     b = got
     a = call(
@@ -274,7 +274,10 @@
     a = shift_x(a)
     a, b, weight, norm_weight = lax.optimization_barrier((a, b, weight, norm_weight))
     a = call(
-        sum_a_kernel, pltpu.VMEM(a_shape, f32), hbm(1) + vmem(3), [pltpu.VMEM(a_shape, f32), dma]
+        sum_a_kernel,
+        pltpu.VMEM(a_shape, f32),
+        hbm(1) + vmem(3),
+        [pltpu.VMEM(a_shape, f32), dma((NZ,))],
     )(*far(a[0]), *near(*a[1:]))
     a = spread(a)
     b = call(
@@ -287,14 +290,17 @@
     a, stepped, stepped_norm = call(
         step_kernel,
         [
-            pltpu.VMEM((NZ, G_ROWS, LANES), bf16),
+            pltpu.VMEM((G_ROWS, LANES), bf16),
             pltpu.VMEM((ROWS, 640), f32),
             pltpu.VMEM((8, LANES), f32),
         ],
         vmem(7),
     )(*near(a, *b, weight, norm_weight))
 
-    a = spread(a)
+    by_step = {0: a}
+    for steps in ((1, 7), (2, 6, 3, 5, 4)):
+        by_step |= {r: shift(a, r, 0) for r in steps}
+    a = jnp.stack([by_step[r] for r in range(NZ)])
     a = shift_x([a] * NX)
     stepped_norm = lax.dynamic_slice_in_dim(stepped_norm[0], 20 * core, 20)
     kept = lax.dynamic_slice_in_dim(stepped, 20 * core, 20)
@@ -307,7 +313,10 @@
     norm = sum(
         jnp.where(own_x == lax.rem(x + NX - j, NX), v[:, None, G_ROWS - 8, :ROWS], 0) for j, v in enumerate(a)
     )
-    scratch = [pltpu.VMEM((640, 640), f32), pltpu.VMEM((640, 1280), bf16), dma((2, 2))]
+    norm = jnp.concatenate([norm[:1], norm[:0:-1]])
+    place = lax.rem(NZ - lax.axis_index("z"), NZ)
+    norm = lax.dynamic_slice_in_dim(jnp.concatenate([norm, norm]), place, NZ)
+    scratch = [pltpu.VMEM((1280, 640), f32), pltpu.VMEM((640, 1280), bf16), dma((2, 2))]
     outs_shape = [FAR((320, 1280), bf16)] * 4
     half = call(partial(turn_kernel, True), outs_shape, vmem(4), scratch, hbm(4))(*near(*a))
     aliases = {4 + i: i for i in range(4)}

time: 122 us -> 141 us (1.16)
  waiting for transfers between devices: 31.1 us -> 62.2 us
  starting transfers between devices: 69.4 us -> 58.2 us
    ppermute x26 -> x33, waiting for transfers between devices: 17.5 us -> 48.6 us  [shift(): return lax.ppermute(v, CHIPS, pairs)]
    ppermute x26 -> x33, starting transfers between devices: 62.3 us -> 51.4 us  [shift(): return lax.ppermute(v, CHIPS, pairs)]
    all_to_all x2 -> x1, starting transfers between devices: 7.09 us -> 6.78 us  [spread(): return lax.all_to_all(v, 'z', 0, 0, tiled=True)]
    all_to_all x2 -> x1, waiting for transfers between devices: 13.6 us -> 13.6 us  [spread(): return lax.all_to_all(v, 'z', 0, 0, tiled=True)]
  transfers between devices with their start and end apart: 28 -> 34, of which waited for: 14 -> 18; matrix products, arithmetic and copies ran while one was open for 2% -> 2% of each run, Pallas kernels for 9% -> 8%
where the time goes in v2:
time: 141 us
  waiting for transfers between devices  62.2 us (44%)
  starting transfers between devices  58.2 us (41%)
  Pallas kernels  16.6 us (12%)
  local copies, waits for them, and re-layouts  2.3 us (2%)
    ppermute x33, starting transfers between devices, shift(): return lax.ppermute(v, CHIPS, pairs)  51.4 us
    ppermute x33, waiting for transfers between devices, shift(): return lax.ppermute(v, CHIPS, pairs)  48.6 us
    all_to_all x1, waiting for transfers between devices, spread(): return lax.all_to_all(v, 'z', 0, 0, tiled=True)  13.6 us
    all_to_all x1, starting transfers between devices, spread(): return lax.all_to_all(v, 'z', 0, 0, tiled=True)  6.78 us
    pallas_call x1, Pallas kernels, on_device(): call(split_a_kernel, [FAR(a_shape, f32)] + [pltpu.VMEM(a_shape, f32)] * 3...  4.43 us
  transfers between devices with their start and end apart: 34, of which 18 were waited for; matrix products, arithmetic and copies ran while one was open for 2% of the time, Pallas kernels for 8%

profile of v2, /device:TPU:1, one launch (start us, length us, event | category | flops | bytes accessed | tf_op | source)
XLA Modules:
  0.0 140.8 jit_solution(16278564838856500693)
XLA Ops:
  0.6 1.9 %shard_map.177 = f32[512,1280]{1,0:T(8,128)S(1)} custom-call(f32[320,1280]{1,0:T(8,128)} %bitcast.48, f32[320,1280]{1,0:T(8,128)} %bitcast.56, f32[320,1280]{1,0:T(8,128)} %bitcast.52, f32[320,1280]{1,0:T(8,128)} %bitcast.58), custom_call_target="tpu_custom_call" | custom-call | tf_op jit(solution)/shard_map/pallas_call | solution.py:241
  2.6 3.3 %collective-permute-start = (f32[512,1280]{1,0:T(8,128)S(1)}, f32[512,1280]{1,0:T(8,128)S(1)}, u32[]{:S(2)}, u32[]{:S(2)}) collective-permute-start(f32[512,1280]{1,0:T(8,128)S(1)} %shard_map.177), channel_id=1, source_target_pairs={{0,4},{4,0},{8,12},{12,8},{16,20},{20,16},{24,28},{28,24},{32,36},... | collective-permute-start | bytes 7864328 | tf_op jit(solution)/shard_map/ppermute | solution.py:29
  7.2 3.2 %collective-permute-done.got = f32[512,1280]{1,0:T(8,128)S(1)} collective-permute-done((f32[512,1280]{1,0:T(8,128)S(1)}, f32[512,1280]{1,0:T(8,128)S(1)}, u32[]{:S(2)}, u32[]{:S(2)}) %collective-permute-start) | collective-permute-done | bytes 2621472 | tf_op jit(solution)/shard_map/ppermute | solution.py:29
  10.4 4.4 %shard_map.178 = (f32[8,160,128]{2,1,0:T(8,128)}, f32[8,160,128]{2,1,0:T(8,128)}, f32[8,160,128]{2,1,0:T(8,128)}, f32[8,160,128]{2,1,0:T(8,128)}) custom-call(f32[320,1280]{1,0:T(8,128)} %bitcast.50, f32[320,1280]{1,0:T(8,128)} %bitcast.57, f32[320,1280]{1,0:T(8,128)} %bitcast.54, f32[320,1280]{1,0:T(8,128)} %bitcast.59, ...), custom_call_target="tpu_custom_call" | custom-call | tf_op jit(solution)/shard_map/pallas_call | solution.py:264
  14.9 2.0 %collective-permute-start.2 = (f32[8,160,128]{2,1,0:T(8,128)}, f32[8,160,128]{2,1,0:T(8,128)S(1)}, u32[]{:S(2)}, u32[]{:S(2)}) collective-permute-start(f32[8,160,128]{2,1,0:T(8,128)} %get-tuple-element.59), channel_id=1, source_target_pairs={{0,16},{4,20},{8,24},{12,28},{16,0},{20,4},{24,8},{28,12},{32,48},... | collective-permute-start | bytes 1966088 | tf_op jit(solution)/shard_map/ppermute | solution.py:29
  20.6 2.4 %shard_map.180 = (f32[4,48,128]{2,1,0:T(8,128)}, f32[4,48,128]{2,1,0:T(8,128)}, f32[4,48,128]{2,1,0:T(8,128)}, f32[4,48,128]{2,1,0:T(8,128)}, f32[4,48,128]{2,1,...) custom-call(f32[320,1280]{1,0:T(8,128)} %bitcast.51, f32[320,1280]{1,0:T(8,128)} %bitcast.55, ...), custom_call_target="tpu_custom_call" | custom-call | tf_op jit(solution)/shard_map/pallas_call | solution.py:253
  23.1 1.7 %collective-permute-start.6 = (f32[4,48,128]{2,1,0:T(8,128)}, f32[4,48,128]{2,1,0:T(8,128)S(1)}, u32[]{:S(2)}, u32[]{:S(2)}) collective-permute-start(f32[4,48,128]{2,1,0:T(8,128)} %get-tuple-element.62), channel_id=1, source_target_pairs={{0,32},{4,36},{8,40},{12,44},{16,48},{20,52},{24,56},{28,60},{32,6... | collective-permute-start | bytes 294920 | tf_op jit(solution)/shard_map/ppermute | solution.py:29
  26.3 3.9 %collective-permute-start.7 = (f32[4,48,128]{2,1,0:T(8,128)}, f32[4,48,128]{2,1,0:T(8,128)S(1)}, u32[]{:S(2)}, u32[]{:S(2)}) collective-permute-start(f32[4,48,128]{2,1,0:T(8,128)} %get-tuple-element.63), channel_id=1, source_target_pairs={{0,224},{4,228},{8,232},{12,236},{16,240},{20,244},{24,248},{28,25... | collective-permute-start | bytes 294920 | tf_op jit(solution)/shard_map/ppermute | solution.py:29
  30.2 1.7 %collective-permute-done.6.refs_1_ = f32[4,48,128]{2,1,0:T(8,128)S(1)} collective-permute-done((f32[4,48,128]{2,1,0:T(8,128)}, f32[4,48,128]{2,1,0:T(8,128)S(1)}, u32[]{:S(2)}, u32[]{:S(2)}) %collective-permute-start.6) | collective-permute-done | bytes 98336 | tf_op jit(solution)/shard_map/ppermute | solution.py:29
  32.5 3.1 %collective-permute-start.9 = (f32[4,48,128]{2,1,0:T(8,128)}, f32[4,48,128]{2,1,0:T(8,128)S(1)}, u32[]{:S(2)}, u32[]{:S(2)}) collective-permute-start(f32[4,48,128]{2,1,0:T(8,128)} %get-tuple-element.65), channel_id=1, source_target_pairs={{0,192},{4,196},{8,200},{12,204},{16,208},{20,212},{24,216},{28,22... | collective-permute-start | bytes 294920 | tf_op jit(solution)/shard_map/ppermute | solution.py:29
  35.6 3.0 %collective-permute-done.8.refs_3_ = f32[4,48,128]{2,1,0:T(8,128)S(1)} collective-permute-done((f32[4,48,128]{2,1,0:T(8,128)}, f32[4,48,128]{2,1,0:T(8,128)S(1)}, u32[]{:S(2)}, u32[]{:S(2)}) %collective-permute-start.8) | collective-permute-done | bytes 98336 | tf_op jit(solution)/shard_map/ppermute | solution.py:29
  39.2 4.2 %collective-permute-start.11 = (f32[4,48,128]{2,1,0:T(8,128)}, f32[4,48,128]{2,1,0:T(8,128)S(1)}, u32[]{:S(2)}, u32[]{:S(2)}) collective-permute-start(f32[4,48,128]{2,1,0:T(8,128)} %get-tuple-element.67), channel_id=1, source_target_pairs={{0,160},{4,164},{8,168},{12,172},{16,176},{20,180},{24,184},{28,18... | collective-permute-start | bytes 294920 | tf_op jit(solution)/shard_map/ppermute | solution.py:29
  43.4 5.0 %collective-permute-done.10.refs_5_ = f32[4,48,128]{2,1,0:T(8,128)S(1)} collective-permute-done((f32[4,48,128]{2,1,0:T(8,128)}, f32[4,48,128]{2,1,0:T(8,128)S(1)}, u32[]{:S(2)}, u32[]{:S(2)}) %collective-permute-start.10) | collective-permute-done | bytes 98336 | tf_op jit(solution)/shard_map/ppermute | solution.py:29
  48.4 4.2 %collective-permute-start.12 = (f32[4,48,128]{2,1,0:T(8,128)}, f32[4,48,128]{2,1,0:T(8,128)S(1)}, u32[]{:S(2)}, u32[]{:S(2)}) collective-permute-start(f32[4,48,128]{2,1,0:T(8,128)} %get-tuple-element.68), channel_id=1, source_target_pairs={{0,128},{4,132},{8,136},{12,140},{16,144},{20,148},{24,152},{28,15... | collective-permute-start | bytes 294920 | tf_op jit(solution)/shard_map/ppermute | solution.py:29
  52.6 3.4 %collective-permute-done.12.refs_7_ = f32[4,48,128]{2,1,0:T(8,128)S(1)} collective-permute-done((f32[4,48,128]{2,1,0:T(8,128)}, f32[4,48,128]{2,1,0:T(8,128)S(1)}, u32[]{:S(2)}, u32[]{:S(2)}) %collective-permute-start.12) | collective-permute-done | bytes 98336 | tf_op jit(solution)/shard_map/ppermute | solution.py:29
  56.0 2.1 %shard_map.181 = f32[8,160,128]{2,1,0:T(8,128)} custom-call(f32[8,160,128]{2,1,0:T(8,128)} %get-tuple-element.69.a0, f32[8,160,128]{2,1,0:T(8,128)S(1)} %collective-permute-done.1.a1, f32[8,160,128]{2,1,0:T(8,128)S(1)} %collective-permute-done.2.a2, f32[8,160,128]{2,1,0:T(8,128)S(1)} %collective-permute-done.3.a3), custom_call_target="tpu_custom_call" | custom-call | tf_op jit(solution)/shard_map/pallas_call | solution.py:276
  58.1 6.8 %all-to-all-start = ((f32[8,160,128]{2,1,0:T(8,128)}), f32[8,160,128]{2,1,0:T(8,128)S(1)}, u32[]{:S(2)}, u32[]{:S(2)}) async-start(f32[8,160,128]{2,1,0:T(8,128)} %shard_map.181), calls=%async_computation | async-start | bytes 1310720 | tf_op jit(solution)/shard_map/all_to_all | solution.py:38
  66.8 2.1 %collective-permute-start.17 = (f32[48,128]{1,0:T(8,128)S(1)}, f32[48,128]{1,0:T(8,128)S(1)}, u32[]{:S(2)}, u32[]{:S(2)}) collective-permute-start(f32[48,128]{1,0:T(8,128)S(1)} %get-tuple-element.84), channel_id=1, source_target_pairs={{0,24},{4,28},{8,0},{12,4},{16,8},{20,12},{24,16},{28,20},{32,56},... | collective-permute-start | bytes 73736 | tf_op jit(solution)/shard_map/ppermute | solution.py:29
  71.0 13.6 %all-to-all-done.a = f32[8,160,128]{2,1,0:T(8,128)S(1)} async-done(((f32[8,160,128]{2,1,0:T(8,128)}), f32[8,160,128]{2,1,0:T(8,128)S(1)}, u32[]{:S(2)}, u32[]{:S(2)}) %all-to-all-start) | async-done | bytes 655392 | tf_op jit(solution)/shard_map/all_to_all | solution.py:38
  84.7 2.0 %collective-permute-start.22 = (bf16[208,128]{1,0:T(8,128)(2,1)S(1)}, bf16[208,128]{1,0:T(8,128)(2,1)S(1)}, u32[]{:S(2)}, u32[]{:S(2)}) collective-permute-start(bf16[208,128]{1,0:T(8,128)(2,1)S(1)} %get-tuple-element.87), channel_id=1, source_target_pairs={{0,160},{4,164},{8,168},{12,172},{16,176},{20,180},{24,184},{28,18... | collective-permute-start | bytes 159752 | tf_op jit(solution)/shard_map/ppermute | solution.py:29
  86.7 3.6 %collective-permute-start.21 = (bf16[208,128]{1,0:T(8,128)(2,1)S(1)}, bf16[208,128]{1,0:T(8,128)(2,1)S(1)}, u32[]{:S(2)}, u32[]{:S(2)}) collective-permute-start(bf16[208,128]{1,0:T(8,128)(2,1)S(1)} %get-tuple-element.87), channel_id=1, source_target_pairs={{0,128},{4,132},{8,136},{12,140},{16,144},{20,148},{24,152},{28,15... | collective-permute-start | bytes 159752 | tf_op jit(solution)/shard_map/ppermute | solution.py:29
  92.2 2.6 %collective-permute-done.18 = bf16[208,128]{1,0:T(8,128)(2,1)S(1)} collective-permute-done((bf16[208,128]{1,0:T(8,128)(2,1)S(1)}, bf16[208,128]{1,0:T(8,128)(2,1)S(1)}, u32[]{:S(2)}, u32[]{:S(2)}) %collective-permute-start.18) | collective-permute-done | bytes 53280 | tf_op jit(solution)/shard_map/ppermute | solution.py:29
  96.0 3.9 %collective-permute-done.19 = bf16[208,128]{1,0:T(8,128)(2,1)S(1)} collective-permute-done((bf16[208,128]{1,0:T(8,128)(2,1)S(1)}, bf16[208,128]{1,0:T(8,128)(2,1)S(1)}, u32[]{:S(2)}, u32[]{:S(2)}) %collective-permute-start.19) | collective-permute-done | bytes 53280 | tf_op jit(solution)/shard_map/ppermute | solution.py:29
  99.9 1.3 collective-permute-start.20
  101.2 4.9 %collective-permute-done.20 = bf16[208,128]{1,0:T(8,128)(2,1)S(1)} collective-permute-done((bf16[208,128]{1,0:T(8,128)(2,1)S(1)}, bf16[208,128]{1,0:T(8,128)(2,1)S(1)}, u32[]{:S(2)}, u32[]{:S(2)}) %collective-permute-start.20) | collective-permute-done | bytes 53280 | tf_op jit(solution)/shard_map/ppermute | solution.py:29
  106.1 6.8 %collective-permute-start.31 = (f32[20,640]{1,0:T(8,128)S(1)}, f32[20,640]{1,0:T(8,128)S(1)}, u32[]{:S(2)}, u32[]{:S(2)}) collective-permute-start(f32[20,640]{1,0:T(8,128)S(1)} %constant_dynamic-slice_fusion.1), channel_id=1, source_target_pairs={{0,4},{4,0},{8,12},{12,8},{16,20},{20,16},{24,28},{28,24},{32,36},... | collective-permute-start | bytes 153608 | tf_op jit(solution)/shard_map/ppermute | solution.py:29
  113.2 2.0 %collective-permute-start.28 = (bf16[8,208,128]{2,1,0:T(8,128)(2,1)S(1)}, bf16[8,208,128]{2,1,0:T(8,128)(2,1)S(1)}, u32[]{:S(2)}, u32[]{:S(2)}) collective-permute-start(bf16[8,208,128]{2,1,0:T(8,128)(2,1)S(1)} %bitcast_dynamic-update-slice_fusion.a0), channel_id=1, source_target_pairs={{0,16},{4,20},{8,24},{12,28},{16,0},{20,4},{24,8},{28,12},{32,48},... | collective-permute-start | bytes 1277960 | tf_op jit(solution)/shard_map/ppermute | solution.py:29
  116.5 8.0 %collective-permute-done.30.a3 = bf16[8,208,128]{2,1,0:T(8,128)(2,1)S(1)} collective-permute-done((bf16[8,208,128]{2,1,0:T(8,128)(2,1)S(1)}, bf16[8,208,128]{2,1,0:T(8,128)(2,1)S(1)}, u32[]{:S(2)}, u32[]{:S(2)}) %collective-permute-start.30) | collective-permute-done | bytes 426016 | tf_op jit(solution)/shard_map/ppermute | solution.py:29
  126.2 1.3 collective-permute-start.29
  127.5 8.1 %collective-permute-done.26.a1 = bf16[8,208,128]{2,1,0:T(8,128)(2,1)S(1)} collective-permute-done((bf16[8,208,128]{2,1,0:T(8,128)(2,1)S(1)}, bf16[8,208,128]{2,1,0:T(8,128)(2,1)S(1)}, u32[]{:S(2)}, u32[]{:S(2)}) %collective-permute-start.26) | collective-permute-done | bytes 426016 | tf_op jit(solution)/shard_map/ppermute | solution.py:29
  137.1 1.7 %shard_map.184 = (bf16[320,1280]{1,0:T(8,128)(2,1)}, bf16[320,1280]{1,0:T(8,128)(2,1)}, bf16[320,1280]{1,0:T(8,128)(2,1)}, bf16[320,1280]{1,0:T(8,128)(2,1)}) custom-call(bf16[8,208,128]{2,1,0:T(8,128)(2,1)S(1)} %bitcast_dynamic-update-slice_fusion.a0, bf16[8,208,128]{2,1,0:T(8,128)(2,1)S(1)} %collective-permute-done.26.a1, ...), custom_call_target="tpu_custom_call" | custom-call | tf_op jit(solution)/shard_map/pallas_call | solution.py:321
  138.9 1.8 %shard_map.185 = (bf16[320,1280]{1,0:T(8,128)(2,1)}, bf16[320,1280]{1,0:T(8,128)(2,1)}, bf16[320,1280]{1,0:T(8,128)(2,1)}, bf16[320,1280]{1,0:T(8,128)(2,1)}) custom-call(bf16[8,208,128]{2,1,0:T(8,128)(2,1)S(1)} %collective-permute-done.25.a0, ...), custom_call_target="tpu_custom_call", output_to_operand_aliasing={{0}: (4, {}), {1}: (5, {}), {2}: (6, {}), {3}: (7, {})} | custom-call | tf_op jit(solution)/shard_map/pallas_call | solution.py:323
  (93 shorter events, 19.5 us)
Async XLA Ops:
  2.6 7.8 %collective-permute-start = (f32[512,1280]{1,0:T(8,128)S(1)}, f32[512,1280]{1,0:T(8,128)S(1)}, u32[]{:S(2)}, u32[]{:S(2)}) collective-permute-start(f32[512,1280]{1,0:T(8,128)S(1)} %shard_map.177), channel_id=1, source_target_pairs={{0,4},{4,0},{8,12},{12,8},{16,20},{20,16},{24,28},{28,24},{32,36},... | collective-permute-start | bytes 7864328 | tf_op jit(solution)/shard_map/ppermute | solution.py:29
  7.1 13.5 %collective-permute-start.4 = (f32[128,1280]{1,0:T(8,128)S(1)}, f32[128,1280]{1,0:T(8,128)S(1)}, u32[]{:S(2)}, u32[]{:S(2)}) collective-permute-start(f32[128,1280]{1,0:T(8,128)S(1)} %shard_map.179), channel_id=1, source_target_pairs={{0,4},{4,0},{8,12},{12,8},{16,20},{20,16},{24,28},{28,24},{32,36},... | collective-permute-start | bytes 1966088 | tf_op jit(solution)/shard_map/ppermute | solution.py:29
  14.8 41.2 %collective-permute-start.1 = (f32[8,160,128]{2,1,0:T(8,128)}, f32[8,160,128]{2,1,0:T(8,128)S(1)}, u32[]{:S(2)}, u32[]{:S(2)}) collective-permute-start(f32[8,160,128]{2,1,0:T(8,128)} %get-tuple-element.58), channel_id=1, source_target_pairs={{0,8},{4,12},{8,16},{12,20},{16,24},{20,28},{24,0},{28,4},{32,40},... | collective-permute-start | bytes 1966088 | tf_op jit(solution)/shard_map/ppermute | solution.py:29
  14.9 41.1 %collective-permute-start.2 = (f32[8,160,128]{2,1,0:T(8,128)}, f32[8,160,128]{2,1,0:T(8,128)S(1)}, u32[]{:S(2)}, u32[]{:S(2)}) collective-permute-start(f32[8,160,128]{2,1,0:T(8,128)} %get-tuple-element.59), channel_id=1, source_target_pairs={{0,16},{4,20},{8,24},{12,28},{16,0},{20,4},{24,8},{28,12},{32,48},... | collective-permute-start | bytes 1966088 | tf_op jit(solution)/shard_map/ppermute | solution.py:29
  16.9 39.1 %collective-permute-start.3 = (f32[8,160,128]{2,1,0:T(8,128)}, f32[8,160,128]{2,1,0:T(8,128)S(1)}, u32[]{:S(2)}, u32[]{:S(2)}) collective-permute-start(f32[8,160,128]{2,1,0:T(8,128)} %get-tuple-element.60), channel_id=1, source_target_pairs={{0,24},{4,28},{8,0},{12,4},{16,8},{20,12},{24,16},{28,20},{32,56},... | collective-permute-start | bytes 1966088 | tf_op jit(solution)/shard_map/ppermute | solution.py:29
  20.1 4.8 %collective-permute-start.14 = (f32[20]{0:T(128)S(1)}, f32[20]{0:T(128)S(1)}, u32[]{:S(2)}, u32[]{:S(2)}) collective-permute-start(f32[20]{0:T(128)S(1)} %copy-done.5), channel_id=1, source_target_pairs={{0,4},{4,0},{8,12},{12,8},{16,20},{20,16},{24,28},{28,24},{32,36},... | collective-permute-start | bytes 248 | tf_op jit(solution)/shard_map/ppermute | solution.py:29
  23.1 8.9 %collective-permute-start.6 = (f32[4,48,128]{2,1,0:T(8,128)}, f32[4,48,128]{2,1,0:T(8,128)S(1)}, u32[]{:S(2)}, u32[]{:S(2)}) collective-permute-start(f32[4,48,128]{2,1,0:T(8,128)} %get-tuple-element.62), channel_id=1, source_target_pairs={{0,32},{4,36},{8,40},{12,44},{16,48},{20,52},{24,56},{28,60},{32,6... | collective-permute-start | bytes 294920 | tf_op jit(solution)/shard_map/ppermute | solution.py:29
  26.3 6.2 %collective-permute-start.7 = (f32[4,48,128]{2,1,0:T(8,128)}, f32[4,48,128]{2,1,0:T(8,128)S(1)}, u32[]{:S(2)}, u32[]{:S(2)}) collective-permute-start(f32[4,48,128]{2,1,0:T(8,128)} %get-tuple-element.63), channel_id=1, source_target_pairs={{0,224},{4,228},{8,232},{12,236},{16,240},{20,244},{24,248},{28,25... | collective-permute-start | bytes 294920 | tf_op jit(solution)/shard_map/ppermute | solution.py:29
  31.9 6.8 %collective-permute-start.8 = (f32[4,48,128]{2,1,0:T(8,128)}, f32[4,48,128]{2,1,0:T(8,128)S(1)}, u32[]{:S(2)}, u32[]{:S(2)}) collective-permute-start(f32[4,48,128]{2,1,0:T(8,128)} %get-tuple-element.64), channel_id=1, source_target_pairs={{0,64},{4,68},{8,72},{12,76},{16,80},{20,84},{24,88},{28,92},{32,9... | collective-permute-start | bytes 294920 | tf_op jit(solution)/shard_map/ppermute | solution.py:29
  32.5 6.7 %collective-permute-start.9 = (f32[4,48,128]{2,1,0:T(8,128)}, f32[4,48,128]{2,1,0:T(8,128)S(1)}, u32[]{:S(2)}, u32[]{:S(2)}) collective-permute-start(f32[4,48,128]{2,1,0:T(8,128)} %get-tuple-element.65), channel_id=1, source_target_pairs={{0,192},{4,196},{8,200},{12,204},{16,208},{20,212},{24,216},{28,22... | collective-permute-start | bytes 294920 | tf_op jit(solution)/shard_map/ppermute | solution.py:29
  38.7 9.7 %collective-permute-start.10 = (f32[4,48,128]{2,1,0:T(8,128)}, f32[4,48,128]{2,1,0:T(8,128)S(1)}, u32[]{:S(2)}, u32[]{:S(2)}) collective-permute-start(f32[4,48,128]{2,1,0:T(8,128)} %get-tuple-element.66), channel_id=1, source_target_pairs={{0,96},{4,100},{8,104},{12,108},{16,112},{20,116},{24,120},{28,124... | collective-permute-start | bytes 294920 | tf_op jit(solution)/shard_map/ppermute | solution.py:29
  39.2 13.4 %collective-permute-start.11 = (f32[4,48,128]{2,1,0:T(8,128)}, f32[4,48,128]{2,1,0:T(8,128)S(1)}, u32[]{:S(2)}, u32[]{:S(2)}) collective-permute-start(f32[4,48,128]{2,1,0:T(8,128)} %get-tuple-element.67), channel_id=1, source_target_pairs={{0,160},{4,164},{8,168},{12,172},{16,176},{20,180},{24,184},{28,18... | collective-permute-start | bytes 294920 | tf_op jit(solution)/shard_map/ppermute | solution.py:29
  48.4 7.6 %collective-permute-start.12 = (f32[4,48,128]{2,1,0:T(8,128)}, f32[4,48,128]{2,1,0:T(8,128)S(1)}, u32[]{:S(2)}, u32[]{:S(2)}) collective-permute-start(f32[4,48,128]{2,1,0:T(8,128)} %get-tuple-element.68), channel_id=1, source_target_pairs={{0,128},{4,132},{8,136},{12,140},{16,144},{20,148},{24,152},{28,15... | collective-permute-start | bytes 294920 | tf_op jit(solution)/shard_map/ppermute | solution.py:29
  58.1 26.4 %all-to-all-start = ((f32[8,160,128]{2,1,0:T(8,128)}), f32[8,160,128]{2,1,0:T(8,128)S(1)}, u32[]{:S(2)}, u32[]{:S(2)}) async-start(f32[8,160,128]{2,1,0:T(8,128)} %shard_map.181), calls=%async_computation | async-start | bytes 1310720 | tf_op jit(solution)/shard_map/all_to_all | solution.py:38
  65.8 4.0 %collective-permute-start.15 = (f32[48,128]{1,0:T(8,128)S(1)}, f32[48,128]{1,0:T(8,128)S(1)}, u32[]{:S(2)}, u32[]{:S(2)}) collective-permute-start(f32[48,128]{1,0:T(8,128)S(1)} %get-tuple-element.82), channel_id=1, source_target_pairs={{0,8},{4,12},{8,16},{12,20},{16,24},{20,28},{24,0},{28,4},{32,40},... | collective-permute-start | bytes 73736 | tf_op jit(solution)/shard_map/ppermute | solution.py:29
  66.4 4.2 %collective-permute-start.16 = (f32[48,128]{1,0:T(8,128)S(1)}, f32[48,128]{1,0:T(8,128)S(1)}, u32[]{:S(2)}, u32[]{:S(2)}) collective-permute-start(f32[48,128]{1,0:T(8,128)S(1)} %get-tuple-element.83), channel_id=1, source_target_pairs={{0,16},{4,20},{8,24},{12,28},{16,0},{20,4},{24,8},{28,12},{32,48},... | collective-permute-start | bytes 73736 | tf_op jit(solution)/shard_map/ppermute | solution.py:29
  66.8 4.1 %collective-permute-start.17 = (f32[48,128]{1,0:T(8,128)S(1)}, f32[48,128]{1,0:T(8,128)S(1)}, u32[]{:S(2)}, u32[]{:S(2)}) collective-permute-start(f32[48,128]{1,0:T(8,128)S(1)} %get-tuple-element.84), channel_id=1, source_target_pairs={{0,24},{4,28},{8,0},{12,4},{16,8},{20,12},{24,16},{28,20},{32,56},... | collective-permute-start | bytes 73736 | tf_op jit(solution)/shard_map/ppermute | solution.py:29
  84.6 28.5 %collective-permute-start.24 = (bf16[208,128]{1,0:T(8,128)(2,1)S(1)}, bf16[208,128]{1,0:T(8,128)(2,1)S(1)}, u32[]{:S(2)}, u32[]{:S(2)}) collective-permute-start(bf16[208,128]{1,0:T(8,128)(2,1)S(1)} %get-tuple-element.87), channel_id=1, source_target_pairs={{0,224},{4,228},{8,232},{12,236},{16,240},{20,244},{24,248},{28,25... | collective-permute-start | bytes 159752 | tf_op jit(solution)/shard_map/ppermute | solution.py:29
  84.7 28.4 %collective-permute-start.23 = (bf16[208,128]{1,0:T(8,128)(2,1)S(1)}, bf16[208,128]{1,0:T(8,128)(2,1)S(1)}, u32[]{:S(2)}, u32[]{:S(2)}) collective-permute-start(bf16[208,128]{1,0:T(8,128)(2,1)S(1)} %get-tuple-element.87), channel_id=1, source_target_pairs={{0,192},{4,196},{8,200},{12,204},{16,208},{20,212},{24,216},{28,22... | collective-permute-start | bytes 159752 | tf_op jit(solution)/shard_map/ppermute | solution.py:29
  84.7 28.3 %collective-permute-start.22 = (bf16[208,128]{1,0:T(8,128)(2,1)S(1)}, bf16[208,128]{1,0:T(8,128)(2,1)S(1)}, u32[]{:S(2)}, u32[]{:S(2)}) collective-permute-start(bf16[208,128]{1,0:T(8,128)(2,1)S(1)} %get-tuple-element.87), channel_id=1, source_target_pairs={{0,160},{4,164},{8,168},{12,172},{16,176},{20,180},{24,184},{28,18... | collective-permute-start | bytes 159752 | tf_op jit(solution)/shard_map/ppermute | solution.py:29
  86.7 26.3 %collective-permute-start.21 = (bf16[208,128]{1,0:T(8,128)(2,1)S(1)}, bf16[208,128]{1,0:T(8,128)(2,1)S(1)}, u32[]{:S(2)}, u32[]{:S(2)}) collective-permute-start(bf16[208,128]{1,0:T(8,128)(2,1)S(1)} %get-tuple-element.87), channel_id=1, source_target_pairs={{0,128},{4,132},{8,136},{12,140},{16,144},{20,148},{24,152},{28,15... | collective-permute-start | bytes 159752 | tf_op jit(solution)/shard_map/ppermute | solution.py:29
  90.3 4.5 %collective-permute-start.18 = (bf16[208,128]{1,0:T(8,128)(2,1)S(1)}, bf16[208,128]{1,0:T(8,128)(2,1)S(1)}, u32[]{:S(2)}, u32[]{:S(2)}) collective-permute-start(bf16[208,128]{1,0:T(8,128)(2,1)S(1)} %get-tuple-element.87), channel_id=1, source_target_pairs={{0,32},{4,36},{8,40},{12,44},{16,48},{20,52},{24,56},{28,60},{32,6... | collective-permute-start | bytes 159752 | tf_op jit(solution)/shard_map/ppermute | solution.py:29
  94.8 5.1 %collective-permute-start.19 = (bf16[208,128]{1,0:T(8,128)(2,1)S(1)}, bf16[208,128]{1,0:T(8,128)(2,1)S(1)}, u32[]{:S(2)}, u32[]{:S(2)}) collective-permute-start(bf16[208,128]{1,0:T(8,128)(2,1)S(1)} %get-tuple-element.87), channel_id=1, source_target_pairs={{0,64},{4,68},{8,72},{12,76},{16,80},{20,84},{24,88},{28,92},{32,9... | collective-permute-start | bytes 159752 | tf_op jit(solution)/shard_map/ppermute | solution.py:29
  99.9 6.2 %collective-permute-start.20 = (bf16[208,128]{1,0:T(8,128)(2,1)S(1)}, bf16[208,128]{1,0:T(8,128)(2,1)S(1)}, u32[]{:S(2)}, u32[]{:S(2)}) collective-permute-start(bf16[208,128]{1,0:T(8,128)(2,1)S(1)} %get-tuple-element.87), channel_id=1, source_target_pairs={{0,96},{4,100},{8,104},{12,108},{16,112},{20,116},{24,120},{28,124... | collective-permute-start | bytes 159752 | tf_op jit(solution)/shard_map/ppermute | solution.py:29
  106.1 9.1 %collective-permute-start.31 = (f32[20,640]{1,0:T(8,128)S(1)}, f32[20,640]{1,0:T(8,128)S(1)}, u32[]{:S(2)}, u32[]{:S(2)}) collective-permute-start(f32[20,640]{1,0:T(8,128)S(1)} %constant_dynamic-slice_fusion.1), channel_id=1, source_target_pairs={{0,4},{4,0},{8,12},{12,8},{16,20},{20,16},{24,28},{28,24},{32,36},... | collective-permute-start | bytes 153608 | tf_op jit(solution)/shard_map/ppermute | solution.py:29
  113.1 11.4 %collective-permute-start.30 = (bf16[8,208,128]{2,1,0:T(8,128)(2,1)S(1)}, bf16[8,208,128]{2,1,0:T(8,128)(2,1)S(1)}, u32[]{:S(2)}, u32[]{:S(2)}) collective-permute-start(bf16[8,208,128]{2,1,0:T(8,128)(2,1)S(1)} %bitcast_dynamic-update-slice_fusion.a0), channel_id=1, source_target_pairs={{0,24},{4,28},{8,0},{12,4},{16,8},{20,12},{24,16},{28,20},{32,56},... | collective-permute-start | bytes 1277960 | tf_op jit(solution)/shard_map/ppermute | solution.py:29
  113.2 13.0 %collective-permute-start.28 = (bf16[8,208,128]{2,1,0:T(8,128)(2,1)S(1)}, bf16[8,208,128]{2,1,0:T(8,128)(2,1)S(1)}, u32[]{:S(2)}, u32[]{:S(2)}) collective-permute-start(bf16[8,208,128]{2,1,0:T(8,128)(2,1)S(1)} %bitcast_dynamic-update-slice_fusion.a0), channel_id=1, source_target_pairs={{0,16},{4,20},{8,24},{12,28},{16,0},{20,4},{24,8},{28,12},{32,48},... | collective-permute-start | bytes 1277960 | tf_op jit(solution)/shard_map/ppermute | solution.py:29
  115.2 20.4 %collective-permute-start.26 = (bf16[8,208,128]{2,1,0:T(8,128)(2,1)S(1)}, bf16[8,208,128]{2,1,0:T(8,128)(2,1)S(1)}, u32[]{:S(2)}, u32[]{:S(2)}) collective-permute-start(bf16[8,208,128]{2,1,0:T(8,128)(2,1)S(1)} %bitcast_dynamic-update-slice_fusion.a0), channel_id=1, source_target_pairs={{0,8},{4,12},{8,16},{12,20},{16,24},{20,28},{24,0},{28,4},{32,40},... | collective-permute-start | bytes 1277960 | tf_op jit(solution)/shard_map/ppermute | solution.py:29
  116.0 22.9 %collective-permute-start.25 = (bf16[8,208,128]{2,1,0:T(8,128)(2,1)S(1)}, bf16[8,208,128]{2,1,0:T(8,128)(2,1)S(1)}, u32[]{:S(2)}, u32[]{:S(2)}) collective-permute-start(bf16[8,208,128]{2,1,0:T(8,128)(2,1)S(1)} %bitcast_dynamic-update-slice_fusion.a0), channel_id=1, source_target_pairs={{0,4},{4,0},{8,12},{12,8},{16,20},{20,16},{24,28},{28,24},{32,36},... | collective-permute-start | bytes 1277960 | tf_op jit(solution)/shard_map/ppermute | solution.py:29
  124.5 14.4 %collective-permute-start.32 = (bf16[8,208,128]{2,1,0:T(8,128)(2,1)S(1)}, bf16[8,208,128]{2,1,0:T(8,128)(2,1)S(1)}, u32[]{:S(2)}, u32[]{:S(2)}) collective-permute-start(bf16[8,208,128]{2,1,0:T(8,128)(2,1)S(1)} %collective-permute-done.30.a3), channel_id=1, source_target_pairs={{0,4},{4,0},{8,12},{12,8},{16,20},{20,16},{24,28},{28,24},{32,36},... | collective-permute-start | bytes 1277960 | tf_op jit(solution)/shard_map/ppermute | solution.py:29
  126.2 12.7 %collective-permute-start.29 = (bf16[8,208,128]{2,1,0:T(8,128)(2,1)S(1)}, bf16[8,208,128]{2,1,0:T(8,128)(2,1)S(1)}, u32[]{:S(2)}, u32[]{:S(2)}) collective-permute-start(bf16[8,208,128]{2,1,0:T(8,128)(2,1)S(1)} %collective-permute-done.28.a2), channel_id=1, source_target_pairs={{0,4},{4,0},{8,12},{12,8},{16,20},{20,16},{24,28},{28,24},{32,36},... | collective-permute-start | bytes 1277960 | tf_op jit(solution)/shard_map/ppermute | solution.py:29
  135.6 3.3 %collective-permute-start.27 = (bf16[8,208,128]{2,1,0:T(8,128)(2,1)S(1)}, bf16[8,208,128]{2,1,0:T(8,128)(2,1)S(1)}, u32[]{:S(2)}, u32[]{:S(2)}) collective-permute-start(bf16[8,208,128]{2,1,0:T(8,128)(2,1)S(1)} %collective-permute-done.26.a1), channel_id=1, source_target_pairs={{0,4},{4,0},{8,12},{12,8},{16,20},{20,16},{24,28},{28,24},{32,36},... | collective-permute-start | bytes 1277960 | tf_op jit(solution)/shard_map/ppermute | solution.py:29
  (8 other events, 44.2 us)

commit v3 on v2

--- a/solution.py
+++ b/solution.py
@@ -34,8 +34,11 @@
     return [v[0], near_ones[0], shift(v[2], 0, 2), near_ones[1]]
 
 
-def spread(v):
-    return lax.all_to_all(v, "z", 0, 0, tiled=True)
+def shift_z(v):
+    out = []
+    for steps in ((1, 7), (2, 6, 3, 5, 4)):
+        out += [shift(v[r], r, 0) for r in steps]
+    return out
 
 
 def block_copies(blocks, out, sems, lanes=pl.ds(0, 1280)):
@@ -136,13 +139,15 @@
     return [pltpu.with_memory_space_constraint(v, pltpu.HBM) for v in arrays]
 
 
-def sum_a_kernel(a0, a1, a2, a3, out, own, sems):
-    copies = [pltpu.make_async_copy(a0.at[z], own.at[z], sems.at[z]) for z in range(NZ)]
+def sum_a_kernel(a0, a1, a2, a3, *refs):
+    *outs, own, sems = refs
+    places = [lax.rem(lax.axis_index("z") + r, NZ) for r in range(NZ)]
+    copies = [pltpu.make_async_copy(a0.at[z], own.at[r], sems.at[r]) for r, z in enumerate(places)]
     for c in copies:
         c.start()
-    for z, c in enumerate(copies):
-        c.wait()
-        out[z] = own[z] + a1[z] + a2[z] + a3[z]
+    for r, z in enumerate(places):
+        copies[r].wait()
+        outs[r][...] = own[r] + a1[z] + a2[z] + a3[z]
 
 
 def sum_b_kernel(*refs):
@@ -159,11 +164,12 @@
         out[...] = total
 
 
-def step_kernel(a, b0, b1, b2, b3, weight, norm_weight, out, stepped, stepped_norm):
+def step_kernel(*refs):
+    a, (b0, b1, b2, b3, weight, norm_weight, out, stepped, stepped_norm) = refs[:NZ], refs[NZ:]
     rate = (NZ * NX * NC) ** (-0.5)
-    total_a = a[0]
-    for z in range(1, NZ):
-        total_a = total_a + a[z]
+    total_a = a[0][...]
+    for r in range(1, NZ):
+        total_a = total_a + a[r][...]
     total_b = b0[...] + b1[...] + b2[...] + b3[...]
     for t in range(COLS):
         lanes = slice(LANES * t, LANES * t + LANES)
@@ -275,18 +281,18 @@
     a, b, weight, norm_weight = lax.optimization_barrier((a, b, weight, norm_weight))
     a = call(
         sum_a_kernel,
-        pltpu.VMEM(a_shape, f32),
+        [pltpu.VMEM((A_ROWS, LANES), f32)] * NZ,
         hbm(1) + vmem(3),
         [pltpu.VMEM(a_shape, f32), dma((NZ,))],
     )(*far(a[0]), *near(*a[1:]))
-    a = spread(a)
+    a = [a[0]] + shift_z(a)
     b = call(
         sum_b_kernel,
         [pltpu.VMEM((B_ROWS, LANES), f32)] * NX,
         hbm(1) + vmem(NZ - 1),
         [pltpu.VMEM(b_shape, f32), dma],
     )(*far(b[0]), *near(*b[1:]))
-    b = [b[0]] + [shift(b[j], 0, j) for j in (1, 2, 3)]
+    b = shift_x(b)
     a, stepped, stepped_norm = call(
         step_kernel,
         [
@@ -294,8 +300,8 @@
             pltpu.VMEM((ROWS, 640), f32),
             pltpu.VMEM((8, LANES), f32),
         ],
-        vmem(7),
-    )(*near(a, *b, weight, norm_weight))
+        vmem(NZ + 6),
+    )(*near(*a, *b, weight, norm_weight))
 
     by_step = {0: a}
     for steps in ((1, 7), (2, 6, 3, 5, 4)):

time: 141 us -> 146 us (1.035)
  starting transfers between devices: 58.2 us -> 70.7 us
  waiting for transfers between devices: 62.2 us -> 55.6 us
    ppermute x33 -> x40, starting transfers between devices: 51.4 us -> 70.7 us  [shift(): return lax.ppermute(v, CHIPS, pairs)]
    all_to_all x1 -> x0, waiting for transfers between devices: 13.6 us -> none  [spread(): return lax.all_to_all(v, 'z', 0, 0, tiled=True)]
    ppermute x33 -> x40, waiting for transfers between devices: 48.6 us -> 55.6 us  [shift(): return lax.ppermute(v, CHIPS, pairs)]
    all_to_all x1 -> x0, starting transfers between devices: 6.78 us -> none  [spread(): return lax.all_to_all(v, 'z', 0, 0, tiled=True)]
  transfers between devices with their start and end apart: 34 -> 40, of which waited for: 18 -> 17; matrix products, arithmetic and copies ran while one was open for 2% -> 2% of each run, Pallas kernels for 8% -> 7%
where the time goes in v3:
time: 146 us
  starting transfers between devices  70.7 us (48%)
  waiting for transfers between devices  55.6 us (38%)
  Pallas kernels  15.7 us (11%)
  local copies, waits for them, and re-layouts  2.3 us (2%)
    ppermute x40, starting transfers between devices, shift(): return lax.ppermute(v, CHIPS, pairs)  70.7 us
    ppermute x40, waiting for transfers between devices, shift(): return lax.ppermute(v, CHIPS, pairs)  55.6 us
    pallas_call x1, Pallas kernels, on_device(): call(split_a_kernel, [FAR(a_shape, f32)] + [pltpu.VMEM(a_shape, f32)] * 3...  4.43 us
  transfers between devices with their start and end apart: 40, of which 17 were waited for; matrix products, arithmetic and copies ran while one was open for 2% of the time, Pallas kernels for 7%

profile of v3, /device:TPU:1, one launch (start us, length us, event | category | flops | bytes accessed | tf_op | source)
XLA Modules:
  0.0 146.1 jit_solution(17540748849479926825)
XLA Ops:
  0.6 1.9 %shard_map.177 = f32[512,1280]{1,0:T(8,128)S(1)} custom-call(f32[320,1280]{1,0:T(8,128)} %bitcast.48, f32[320,1280]{1,0:T(8,128)} %bitcast.56, f32[320,1280]{1,0:T(8,128)} %bitcast.52, f32[320,1280]{1,0:T(8,128)} %bitcast.58), custom_call_target="tpu_custom_call" | custom-call | tf_op jit(solution)/shard_map/pallas_call | solution.py:247
  2.6 3.3 %collective-permute-start = (f32[512,1280]{1,0:T(8,128)S(1)}, f32[512,1280]{1,0:T(8,128)S(1)}, u32[]{:S(2)}, u32[]{:S(2)}) collective-permute-start(f32[512,1280]{1,0:T(8,128)S(1)} %shard_map.177), channel_id=1, source_target_pairs={{0,4},{4,0},{8,12},{12,8},{16,20},{20,16},{24,28},{28,24},{32,36},... | collective-permute-start | bytes 7864328 | tf_op jit(solution)/shard_map/ppermute | solution.py:29
  7.2 3.2 %collective-permute-done.got = f32[512,1280]{1,0:T(8,128)S(1)} collective-permute-done((f32[512,1280]{1,0:T(8,128)S(1)}, f32[512,1280]{1,0:T(8,128)S(1)}, u32[]{:S(2)}, u32[]{:S(2)}) %collective-permute-start) | collective-permute-done | bytes 2621472 | tf_op jit(solution)/shard_map/ppermute | solution.py:29
  10.4 4.4 %shard_map.178 = (f32[8,160,128]{2,1,0:T(8,128)}, f32[8,160,128]{2,1,0:T(8,128)}, f32[8,160,128]{2,1,0:T(8,128)}, f32[8,160,128]{2,1,0:T(8,128)}) custom-call(f32[320,1280]{1,0:T(8,128)} %bitcast.50, f32[320,1280]{1,0:T(8,128)} %bitcast.57, f32[320,1280]{1,0:T(8,128)} %bitcast.54, f32[320,1280]{1,0:T(8,128)} %bitcast.59, ...), custom_call_target="tpu_custom_call" | custom-call | tf_op jit(solution)/shard_map/pallas_call | solution.py:270
  14.9 2.0 %collective-permute-start.2 = (f32[8,160,128]{2,1,0:T(8,128)}, f32[8,160,128]{2,1,0:T(8,128)S(1)}, u32[]{:S(2)}, u32[]{:S(2)}) collective-permute-start(f32[8,160,128]{2,1,0:T(8,128)} %get-tuple-element.67), channel_id=1, source_target_pairs={{0,16},{4,20},{8,24},{12,28},{16,0},{20,4},{24,8},{28,12},{32,48},... | collective-permute-start | bytes 1966088 | tf_op jit(solution)/shard_map/ppermute | solution.py:29
  20.6 2.4 %shard_map.180 = (f32[4,48,128]{2,1,0:T(8,128)}, f32[4,48,128]{2,1,0:T(8,128)}, f32[4,48,128]{2,1,0:T(8,128)}, f32[4,48,128]{2,1,0:T(8,128)}, f32[4,48,128]{2,1,...) custom-call(f32[320,1280]{1,0:T(8,128)} %bitcast.51, f32[320,1280]{1,0:T(8,128)} %bitcast.55, ...), custom_call_target="tpu_custom_call" | custom-call | tf_op jit(solution)/shard_map/pallas_call | solution.py:259
  26.3 3.9 %collective-permute-start.7 = (f32[4,48,128]{2,1,0:T(8,128)}, f32[4,48,128]{2,1,0:T(8,128)S(1)}, u32[]{:S(2)}, u32[]{:S(2)}) collective-permute-start(f32[4,48,128]{2,1,0:T(8,128)} %get-tuple-element.71), channel_id=1, source_target_pairs={{0,224},{4,228},{8,232},{12,236},{16,240},{20,244},{24,248},{28,25... | collective-permute-start | bytes 294920 | tf_op jit(solution)/shard_map/ppermute | solution.py:29
  32.5 3.1 %collective-permute-start.9 = (f32[4,48,128]{2,1,0:T(8,128)}, f32[4,48,128]{2,1,0:T(8,128)S(1)}, u32[]{:S(2)}, u32[]{:S(2)}) collective-permute-start(f32[4,48,128]{2,1,0:T(8,128)} %get-tuple-element.73), channel_id=1, source_target_pairs={{0,192},{4,196},{8,200},{12,204},{16,208},{20,212},{24,216},{28,22... | collective-permute-start | bytes 294920 | tf_op jit(solution)/shard_map/ppermute | solution.py:29
  35.6 3.0 %collective-permute-done.8.refs_3_ = f32[4,48,128]{2,1,0:T(8,128)S(1)} collective-permute-done((f32[4,48,128]{2,1,0:T(8,128)}, f32[4,48,128]{2,1,0:T(8,128)S(1)}, u32[]{:S(2)}, u32[]{:S(2)}) %collective-permute-start.8) | collective-permute-done | bytes 98336 | tf_op jit(solution)/shard_map/ppermute | solution.py:29
  39.2 4.2 %collective-permute-start.11 = (f32[4,48,128]{2,1,0:T(8,128)}, f32[4,48,128]{2,1,0:T(8,128)S(1)}, u32[]{:S(2)}, u32[]{:S(2)}) collective-permute-start(f32[4,48,128]{2,1,0:T(8,128)} %get-tuple-element.75), channel_id=1, source_target_pairs={{0,160},{4,164},{8,168},{12,172},{16,176},{20,180},{24,184},{28,18... | collective-permute-start | bytes 294920 | tf_op jit(solution)/shard_map/ppermute | solution.py:29
  43.4 5.0 %collective-permute-done.10.refs_5_ = f32[4,48,128]{2,1,0:T(8,128)S(1)} collective-permute-done((f32[4,48,128]{2,1,0:T(8,128)}, f32[4,48,128]{2,1,0:T(8,128)S(1)}, u32[]{:S(2)}, u32[]{:S(2)}) %collective-permute-start.10) | collective-permute-done | bytes 98336 | tf_op jit(solution)/shard_map/ppermute | solution.py:29
  48.4 4.2 %collective-permute-start.12 = (f32[4,48,128]{2,1,0:T(8,128)}, f32[4,48,128]{2,1,0:T(8,128)S(1)}, u32[]{:S(2)}, u32[]{:S(2)}) collective-permute-start(f32[4,48,128]{2,1,0:T(8,128)} %get-tuple-element.76), channel_id=1, source_target_pairs={{0,128},{4,132},{8,136},{12,140},{16,144},{20,148},{24,152},{28,15... | collective-permute-start | bytes 294920 | tf_op jit(solution)/shard_map/ppermute | solution.py:29
  52.6 3.4 %collective-permute-done.12.refs_7_ = f32[4,48,128]{2,1,0:T(8,128)S(1)} collective-permute-done((f32[4,48,128]{2,1,0:T(8,128)}, f32[4,48,128]{2,1,0:T(8,128)S(1)}, u32[]{:S(2)}, u32[]{:S(2)}) %collective-permute-start.12) | collective-permute-done | bytes 98336 | tf_op jit(solution)/shard_map/ppermute | solution.py:29
  57.8 2.2 %collective-permute-start.16 = (f32[160,128]{1,0:T(8,128)S(1)}, f32[160,128]{1,0:T(8,128)S(1)}, u32[]{:S(2)}, u32[]{:S(2)}) collective-permute-start(f32[160,128]{1,0:T(8,128)S(1)} %get-tuple-element.83), channel_id=1, source_target_pairs={{0,224},{4,228},{8,232},{12,236},{16,240},{20,244},{24,248},{28,25... | collective-permute-start | bytes 245768 | tf_op jit(solution)/shard_map/ppermute | solution.py:29
  62.0 2.0 %collective-permute-start.24 = (f32[48,128]{1,0:T(8,128)S(1)}, f32[48,128]{1,0:T(8,128)S(1)}, u32[]{:S(2)}, u32[]{:S(2)}) collective-permute-start(f32[48,128]{1,0:T(8,128)S(1)} %get-tuple-element.100), channel_id=1, source_target_pairs={{0,24},{4,28},{8,0},{12,4},{16,8},{20,12},{24,16},{28,20},{32,56},... | collective-permute-start | bytes 73736 | tf_op jit(solution)/shard_map/ppermute | solution.py:29
  65.6 3.0 %collective-permute-start.18 = (f32[160,128]{1,0:T(8,128)S(1)}, f32[160,128]{1,0:T(8,128)S(1)}, u32[]{:S(2)}, u32[]{:S(2)}) collective-permute-start(f32[160,128]{1,0:T(8,128)S(1)} %get-tuple-element.85), channel_id=1, source_target_pairs={{0,192},{4,196},{8,200},{12,204},{16,208},{20,212},{24,216},{28,22... | collective-permute-start | bytes 245768 | tf_op jit(solution)/shard_map/ppermute | solution.py:29
  68.6 1.8 %collective-permute-start.19 = (f32[160,128]{1,0:T(8,128)S(1)}, f32[160,128]{1,0:T(8,128)S(1)}, u32[]{:S(2)}, u32[]{:S(2)}) collective-permute-start(f32[160,128]{1,0:T(8,128)S(1)} %get-tuple-element.86), channel_id=1, source_target_pairs={{0,96},{4,100},{8,104},{12,108},{16,112},{20,116},{24,120},{28,124... | collective-permute-start | bytes 245768 | tf_op jit(solution)/shard_map/ppermute | solution.py:29
  70.5 2.7 %collective-permute-start.20 = (f32[160,128]{1,0:T(8,128)S(1)}, f32[160,128]{1,0:T(8,128)S(1)}, u32[]{:S(2)}, u32[]{:S(2)}) collective-permute-start(f32[160,128]{1,0:T(8,128)S(1)} %get-tuple-element.87), channel_id=1, source_target_pairs={{0,160},{4,164},{8,168},{12,172},{16,176},{20,180},{24,184},{28,18... | collective-permute-start | bytes 245768 | tf_op jit(solution)/shard_map/ppermute | solution.py:29
  73.1 5.4 %collective-permute-start.21 = (f32[160,128]{1,0:T(8,128)S(1)}, f32[160,128]{1,0:T(8,128)S(1)}, u32[]{:S(2)}, u32[]{:S(2)}) collective-permute-start(f32[160,128]{1,0:T(8,128)S(1)} %get-tuple-element.88), channel_id=1, source_target_pairs={{0,128},{4,132},{8,136},{12,140},{16,144},{20,148},{24,152},{28,15... | collective-permute-start | bytes 245768 | tf_op jit(solution)/shard_map/ppermute | solution.py:29
  78.6 3.1 %collective-permute-done.21.refs_7_ = f32[160,128]{1,0:T(8,128)S(1)} collective-permute-done((f32[160,128]{1,0:T(8,128)S(1)}, f32[160,128]{1,0:T(8,128)S(1)}, u32[]{:S(2)}, u32[]{:S(2)}) %collective-permute-start.21) | collective-permute-done | bytes 81952 | tf_op jit(solution)/shard_map/ppermute | solution.py:29
  81.7 2.2 %collective-permute-start.31 = (bf16[208,128]{1,0:T(8,128)(2,1)S(1)}, bf16[208,128]{1,0:T(8,128)(2,1)S(1)}, u32[]{:S(2)}, u32[]{:S(2)}) collective-permute-start(bf16[208,128]{1,0:T(8,128)(2,1)S(1)} %get-tuple-element.103), channel_id=1, source_target_pairs={{0,224},{4,228},{8,232},{12,236},{16,240},{20,244},{24,248},{28,25... | collective-permute-start | bytes 159752 | tf_op jit(solution)/shard_map/ppermute | solution.py:29
  83.9 5.0 %collective-permute-start.30 = (bf16[208,128]{1,0:T(8,128)(2,1)S(1)}, bf16[208,128]{1,0:T(8,128)(2,1)S(1)}, u32[]{:S(2)}, u32[]{:S(2)}) collective-permute-start(bf16[208,128]{1,0:T(8,128)(2,1)S(1)} %get-tuple-element.103), channel_id=1, source_target_pairs={{0,192},{4,196},{8,200},{12,204},{16,208},{20,212},{24,216},{28,22... | collective-permute-start | bytes 159752 | tf_op jit(solution)/shard_map/ppermute | solution.py:29
  89.1 2.7 %collective-permute-start.28 = (bf16[208,128]{1,0:T(8,128)(2,1)S(1)}, bf16[208,128]{1,0:T(8,128)(2,1)S(1)}, u32[]{:S(2)}, u32[]{:S(2)}) collective-permute-start(bf16[208,128]{1,0:T(8,128)(2,1)S(1)} %get-tuple-element.103), channel_id=1, source_target_pairs={{0,128},{4,132},{8,136},{12,140},{16,144},{20,148},{24,152},{28,15... | collective-permute-start | bytes 159752 | tf_op jit(solution)/shard_map/ppermute | solution.py:29
  93.5 3.8 %collective-permute-done.25 = bf16[208,128]{1,0:T(8,128)(2,1)S(1)} collective-permute-done((bf16[208,128]{1,0:T(8,128)(2,1)S(1)}, bf16[208,128]{1,0:T(8,128)(2,1)S(1)}, u32[]{:S(2)}, u32[]{:S(2)}) %collective-permute-start.25) | collective-permute-done | bytes 53280 | tf_op jit(solution)/shard_map/ppermute | solution.py:29
  97.3 5.1 %collective-permute-done.26 = bf16[208,128]{1,0:T(8,128)(2,1)S(1)} collective-permute-done((bf16[208,128]{1,0:T(8,128)(2,1)S(1)}, bf16[208,128]{1,0:T(8,128)(2,1)S(1)}, u32[]{:S(2)}, u32[]{:S(2)}) %collective-permute-start.26) | collective-permute-done | bytes 53280 | tf_op jit(solution)/shard_map/ppermute | solution.py:29
  102.8 6.1 %collective-permute-done.27 = bf16[208,128]{1,0:T(8,128)(2,1)S(1)} collective-permute-done((bf16[208,128]{1,0:T(8,128)(2,1)S(1)}, bf16[208,128]{1,0:T(8,128)(2,1)S(1)}, u32[]{:S(2)}, u32[]{:S(2)}) %collective-permute-start.27) | collective-permute-done | bytes 53280 | tf_op jit(solution)/shard_map/ppermute | solution.py:29
  108.8 8.5 %collective-permute-start.38 = (f32[20,640]{1,0:T(8,128)S(1)}, f32[20,640]{1,0:T(8,128)S(1)}, u32[]{:S(2)}, u32[]{:S(2)}) collective-permute-start(f32[20,640]{1,0:T(8,128)S(1)} %constant_dynamic-slice_fusion.1), channel_id=1, source_target_pairs={{0,4},{4,0},{8,12},{12,8},{16,20},{20,16},{24,28},{28,24},{32,36},... | collective-permute-start | bytes 153608 | tf_op jit(solution)/shard_map/ppermute | solution.py:29
  120.5 8.4 %collective-permute-done.37.a3 = bf16[8,208,128]{2,1,0:T(8,128)(2,1)S(1)} collective-permute-done((bf16[8,208,128]{2,1,0:T(8,128)(2,1)S(1)}, bf16[8,208,128]{2,1,0:T(8,128)(2,1)S(1)}, u32[]{:S(2)}, u32[]{:S(2)}) %collective-permute-start.37) | collective-permute-done | bytes 426016 | tf_op jit(solution)/shard_map/ppermute | solution.py:29
  131.1 1.9 %collective-permute-start.36 = (bf16[8,208,128]{2,1,0:T(8,128)(2,1)S(1)}, bf16[8,208,128]{2,1,0:T(8,128)(2,1)S(1)}, u32[]{:S(2)}, u32[]{:S(2)}) collective-permute-start(bf16[8,208,128]{2,1,0:T(8,128)(2,1)S(1)} %collective-permute-done.35.a2), channel_id=1, source_target_pairs={{0,4},{4,0},{8,12},{12,8},{16,20},{20,16},{24,28},{28,24},{32,36},... | collective-permute-start | bytes 1277960 | tf_op jit(solution)/shard_map/ppermute | solution.py:29
  133.0 7.8 %collective-permute-done.33.a1 = bf16[8,208,128]{2,1,0:T(8,128)(2,1)S(1)} collective-permute-done((bf16[8,208,128]{2,1,0:T(8,128)(2,1)S(1)}, bf16[8,208,128]{2,1,0:T(8,128)(2,1)S(1)}, u32[]{:S(2)}, u32[]{:S(2)}) %collective-permute-start.33) | collective-permute-done | bytes 426016 | tf_op jit(solution)/shard_map/ppermute | solution.py:29
  142.3 1.7 %shard_map.184 = (bf16[320,1280]{1,0:T(8,128)(2,1)}, bf16[320,1280]{1,0:T(8,128)(2,1)}, bf16[320,1280]{1,0:T(8,128)(2,1)}, bf16[320,1280]{1,0:T(8,128)(2,1)}) custom-call(bf16[8,208,128]{2,1,0:T(8,128)(2,1)S(1)} %bitcast_dynamic-update-slice_fusion.a0, bf16[8,208,128]{2,1,0:T(8,128)(2,1)S(1)} %collective-permute-done.33.a1, ...), custom_call_target="tpu_custom_call" | custom-call | tf_op jit(solution)/shard_map/pallas_call | solution.py:327
  144.1 1.8 %shard_map.185 = (bf16[320,1280]{1,0:T(8,128)(2,1)}, bf16[320,1280]{1,0:T(8,128)(2,1)}, bf16[320,1280]{1,0:T(8,128)(2,1)}, bf16[320,1280]{1,0:T(8,128)(2,1)}) custom-call(bf16[8,208,128]{2,1,0:T(8,128)(2,1)S(1)} %collective-permute-done.32.a0, ...), custom_call_target="tpu_custom_call", output_to_operand_aliasing={{0}: (4, {}), {1}: (5, {}), {2}: (6, {}), {3}: (7, {})} | custom-call | tf_op jit(solution)/shard_map/pallas_call | solution.py:329
  (105 shorter events, 25.7 us)
Async XLA Ops:
  2.6 7.8 %collective-permute-start = (f32[512,1280]{1,0:T(8,128)S(1)}, f32[512,1280]{1,0:T(8,128)S(1)}, u32[]{:S(2)}, u32[]{:S(2)}) collective-permute-start(f32[512,1280]{1,0:T(8,128)S(1)} %shard_map.177), channel_id=1, source_target_pairs={{0,4},{4,0},{8,12},{12,8},{16,20},{20,16},{24,28},{28,24},{32,36},... | collective-permute-start | bytes 7864328 | tf_op jit(solution)/shard_map/ppermute | solution.py:29
  7.1 13.5 %collective-permute-start.4 = (f32[128,1280]{1,0:T(8,128)S(1)}, f32[128,1280]{1,0:T(8,128)S(1)}, u32[]{:S(2)}, u32[]{:S(2)}) collective-permute-start(f32[128,1280]{1,0:T(8,128)S(1)} %shard_map.179), channel_id=1, source_target_pairs={{0,4},{4,0},{8,12},{12,8},{16,20},{20,16},{24,28},{28,24},{32,36},... | collective-permute-start | bytes 1966088 | tf_op jit(solution)/shard_map/ppermute | solution.py:29
  14.8 41.2 %collective-permute-start.1 = (f32[8,160,128]{2,1,0:T(8,128)}, f32[8,160,128]{2,1,0:T(8,128)S(1)}, u32[]{:S(2)}, u32[]{:S(2)}) collective-permute-start(f32[8,160,128]{2,1,0:T(8,128)} %get-tuple-element.66), channel_id=1, source_target_pairs={{0,8},{4,12},{8,16},{12,20},{16,24},{20,28},{24,0},{28,4},{32,40},... | collective-permute-start | bytes 1966088 | tf_op jit(solution)/shard_map/ppermute | solution.py:29
  14.9 41.1 %collective-permute-start.2 = (f32[8,160,128]{2,1,0:T(8,128)}, f32[8,160,128]{2,1,0:T(8,128)S(1)}, u32[]{:S(2)}, u32[]{:S(2)}) collective-permute-start(f32[8,160,128]{2,1,0:T(8,128)} %get-tuple-element.67), channel_id=1, source_target_pairs={{0,16},{4,20},{8,24},{12,28},{16,0},{20,4},{24,8},{28,12},{32,48},... | collective-permute-start | bytes 1966088 | tf_op jit(solution)/shard_map/ppermute | solution.py:29
  16.9 39.1 %collective-permute-start.3 = (f32[8,160,128]{2,1,0:T(8,128)}, f32[8,160,128]{2,1,0:T(8,128)S(1)}, u32[]{:S(2)}, u32[]{:S(2)}) collective-permute-start(f32[8,160,128]{2,1,0:T(8,128)} %get-tuple-element.68), channel_id=1, source_target_pairs={{0,24},{4,28},{8,0},{12,4},{16,8},{20,12},{24,16},{28,20},{32,56},... | collective-permute-start | bytes 1966088 | tf_op jit(solution)/shard_map/ppermute | solution.py:29
  23.1 8.9 %collective-permute-start.6 = (f32[4,48,128]{2,1,0:T(8,128)}, f32[4,48,128]{2,1,0:T(8,128)S(1)}, u32[]{:S(2)}, u32[]{:S(2)}) collective-permute-start(f32[4,48,128]{2,1,0:T(8,128)} %get-tuple-element.70), channel_id=1, source_target_pairs={{0,32},{4,36},{8,40},{12,44},{16,48},{20,52},{24,56},{28,60},{32,6... | collective-permute-start | bytes 294920 | tf_op jit(solution)/shard_map/ppermute | solution.py:29
  26.3 6.2 %collective-permute-start.7 = (f32[4,48,128]{2,1,0:T(8,128)}, f32[4,48,128]{2,1,0:T(8,128)S(1)}, u32[]{:S(2)}, u32[]{:S(2)}) collective-permute-start(f32[4,48,128]{2,1,0:T(8,128)} %get-tuple-element.71), channel_id=1, source_target_pairs={{0,224},{4,228},{8,232},{12,236},{16,240},{20,244},{24,248},{28,25... | collective-permute-start | bytes 294920 | tf_op jit(solution)/shard_map/ppermute | solution.py:29
  31.9 6.8 %collective-permute-start.8 = (f32[4,48,128]{2,1,0:T(8,128)}, f32[4,48,128]{2,1,0:T(8,128)S(1)}, u32[]{:S(2)}, u32[]{:S(2)}) collective-permute-start(f32[4,48,128]{2,1,0:T(8,128)} %get-tuple-element.72), channel_id=1, source_target_pairs={{0,64},{4,68},{8,72},{12,76},{16,80},{20,84},{24,88},{28,92},{32,9... | collective-permute-start | bytes 294920 | tf_op jit(solution)/shard_map/ppermute | solution.py:29
  32.5 6.7 %collective-permute-start.9 = (f32[4,48,128]{2,1,0:T(8,128)}, f32[4,48,128]{2,1,0:T(8,128)S(1)}, u32[]{:S(2)}, u32[]{:S(2)}) collective-permute-start(f32[4,48,128]{2,1,0:T(8,128)} %get-tuple-element.73), channel_id=1, source_target_pairs={{0,192},{4,196},{8,200},{12,204},{16,208},{20,212},{24,216},{28,22... | collective-permute-start | bytes 294920 | tf_op jit(solution)/shard_map/ppermute | solution.py:29
  38.7 9.7 %collective-permute-start.10 = (f32[4,48,128]{2,1,0:T(8,128)}, f32[4,48,128]{2,1,0:T(8,128)S(1)}, u32[]{:S(2)}, u32[]{:S(2)}) collective-permute-start(f32[4,48,128]{2,1,0:T(8,128)} %get-tuple-element.74), channel_id=1, source_target_pairs={{0,96},{4,100},{8,104},{12,108},{16,112},{20,116},{24,120},{28,124... | collective-permute-start | bytes 294920 | tf_op jit(solution)/shard_map/ppermute | solution.py:29
  39.2 13.4 %collective-permute-start.11 = (f32[4,48,128]{2,1,0:T(8,128)}, f32[4,48,128]{2,1,0:T(8,128)S(1)}, u32[]{:S(2)}, u32[]{:S(2)}) collective-permute-start(f32[4,48,128]{2,1,0:T(8,128)} %get-tuple-element.75), channel_id=1, source_target_pairs={{0,160},{4,164},{8,168},{12,172},{16,176},{20,180},{24,184},{28,18... | collective-permute-start | bytes 294920 | tf_op jit(solution)/shard_map/ppermute | solution.py:29
  48.4 7.6 %collective-permute-start.12 = (f32[4,48,128]{2,1,0:T(8,128)}, f32[4,48,128]{2,1,0:T(8,128)S(1)}, u32[]{:S(2)}, u32[]{:S(2)}) collective-permute-start(f32[4,48,128]{2,1,0:T(8,128)} %get-tuple-element.76), channel_id=1, source_target_pairs={{0,128},{4,132},{8,136},{12,140},{16,144},{20,148},{24,152},{28,15... | collective-permute-start | bytes 294920 | tf_op jit(solution)/shard_map/ppermute | solution.py:29
  57.3 13.2 %collective-permute-start.15 = (f32[160,128]{1,0:T(8,128)S(1)}, f32[160,128]{1,0:T(8,128)S(1)}, u32[]{:S(2)}, u32[]{:S(2)}) collective-permute-start(f32[160,128]{1,0:T(8,128)S(1)} %get-tuple-element.82), channel_id=1, source_target_pairs={{0,32},{4,36},{8,40},{12,44},{16,48},{20,52},{24,56},{28,60},{32,6... | collective-permute-start | bytes 245768 | tf_op jit(solution)/shard_map/ppermute | solution.py:29
  57.8 15.3 %collective-permute-start.16 = (f32[160,128]{1,0:T(8,128)S(1)}, f32[160,128]{1,0:T(8,128)S(1)}, u32[]{:S(2)}, u32[]{:S(2)}) collective-permute-start(f32[160,128]{1,0:T(8,128)S(1)} %get-tuple-element.83), channel_id=1, source_target_pairs={{0,224},{4,228},{8,232},{12,236},{16,240},{20,244},{24,248},{28,25... | collective-permute-start | bytes 245768 | tf_op jit(solution)/shard_map/ppermute | solution.py:29
  62.0 6.7 %collective-permute-start.24 = (f32[48,128]{1,0:T(8,128)S(1)}, f32[48,128]{1,0:T(8,128)S(1)}, u32[]{:S(2)}, u32[]{:S(2)}) collective-permute-start(f32[48,128]{1,0:T(8,128)S(1)} %get-tuple-element.100), channel_id=1, source_target_pairs={{0,24},{4,28},{8,0},{12,4},{16,8},{20,12},{24,16},{28,20},{32,56},... | collective-permute-start | bytes 73736 | tf_op jit(solution)/shard_map/ppermute | solution.py:29
  65.1 13.5 %collective-permute-start.17 = (f32[160,128]{1,0:T(8,128)S(1)}, f32[160,128]{1,0:T(8,128)S(1)}, u32[]{:S(2)}, u32[]{:S(2)}) collective-permute-start(f32[160,128]{1,0:T(8,128)S(1)} %get-tuple-element.84), channel_id=1, source_target_pairs={{0,64},{4,68},{8,72},{12,76},{16,80},{20,84},{24,88},{28,92},{32,9... | collective-permute-start | bytes 245768 | tf_op jit(solution)/shard_map/ppermute | solution.py:29
  65.6 12.9 %collective-permute-start.18 = (f32[160,128]{1,0:T(8,128)S(1)}, f32[160,128]{1,0:T(8,128)S(1)}, u32[]{:S(2)}, u32[]{:S(2)}) collective-permute-start(f32[160,128]{1,0:T(8,128)S(1)} %get-tuple-element.85), channel_id=1, source_target_pairs={{0,192},{4,196},{8,200},{12,204},{16,208},{20,212},{24,216},{28,22... | collective-permute-start | bytes 245768 | tf_op jit(solution)/shard_map/ppermute | solution.py:29
  68.6 9.9 %collective-permute-start.19 = (f32[160,128]{1,0:T(8,128)S(1)}, f32[160,128]{1,0:T(8,128)S(1)}, u32[]{:S(2)}, u32[]{:S(2)}) collective-permute-start(f32[160,128]{1,0:T(8,128)S(1)} %get-tuple-element.86), channel_id=1, source_target_pairs={{0,96},{4,100},{8,104},{12,108},{16,112},{20,116},{24,120},{28,124... | collective-permute-start | bytes 245768 | tf_op jit(solution)/shard_map/ppermute | solution.py:29
  70.5 8.1 %collective-permute-start.20 = (f32[160,128]{1,0:T(8,128)S(1)}, f32[160,128]{1,0:T(8,128)S(1)}, u32[]{:S(2)}, u32[]{:S(2)}) collective-permute-start(f32[160,128]{1,0:T(8,128)S(1)} %get-tuple-element.87), channel_id=1, source_target_pairs={{0,160},{4,164},{8,168},{12,172},{16,176},{20,180},{24,184},{28,18... | collective-permute-start | bytes 245768 | tf_op jit(solution)/shard_map/ppermute | solution.py:29
  73.1 8.5 %collective-permute-start.21 = (f32[160,128]{1,0:T(8,128)S(1)}, f32[160,128]{1,0:T(8,128)S(1)}, u32[]{:S(2)}, u32[]{:S(2)}) collective-permute-start(f32[160,128]{1,0:T(8,128)S(1)} %get-tuple-element.88), channel_id=1, source_target_pairs={{0,128},{4,132},{8,136},{12,140},{16,144},{20,148},{24,152},{28,15... | collective-permute-start | bytes 245768 | tf_op jit(solution)/shard_map/ppermute | solution.py:29
  81.7 35.7 %collective-permute-start.31 = (bf16[208,128]{1,0:T(8,128)(2,1)S(1)}, bf16[208,128]{1,0:T(8,128)(2,1)S(1)}, u32[]{:S(2)}, u32[]{:S(2)}) collective-permute-start(bf16[208,128]{1,0:T(8,128)(2,1)S(1)} %get-tuple-element.103), channel_id=1, source_target_pairs={{0,224},{4,228},{8,232},{12,236},{16,240},{20,244},{24,248},{28,25... | collective-permute-start | bytes 159752 | tf_op jit(solution)/shard_map/ppermute | solution.py:29
  83.9 33.5 %collective-permute-start.30 = (bf16[208,128]{1,0:T(8,128)(2,1)S(1)}, bf16[208,128]{1,0:T(8,128)(2,1)S(1)}, u32[]{:S(2)}, u32[]{:S(2)}) collective-permute-start(bf16[208,128]{1,0:T(8,128)(2,1)S(1)} %get-tuple-element.103), channel_id=1, source_target_pairs={{0,192},{4,196},{8,200},{12,204},{16,208},{20,212},{24,216},{28,22... | collective-permute-start | bytes 159752 | tf_op jit(solution)/shard_map/ppermute | solution.py:29
  88.9 28.4 %collective-permute-start.29 = (bf16[208,128]{1,0:T(8,128)(2,1)S(1)}, bf16[208,128]{1,0:T(8,128)(2,1)S(1)}, u32[]{:S(2)}, u32[]{:S(2)}) collective-permute-start(bf16[208,128]{1,0:T(8,128)(2,1)S(1)} %get-tuple-element.103), channel_id=1, source_target_pairs={{0,160},{4,164},{8,168},{12,172},{16,176},{20,180},{24,184},{28,18... | collective-permute-start | bytes 159752 | tf_op jit(solution)/shard_map/ppermute | solution.py:29
  89.1 28.3 %collective-permute-start.28 = (bf16[208,128]{1,0:T(8,128)(2,1)S(1)}, bf16[208,128]{1,0:T(8,128)(2,1)S(1)}, u32[]{:S(2)}, u32[]{:S(2)}) collective-permute-start(bf16[208,128]{1,0:T(8,128)(2,1)S(1)} %get-tuple-element.103), channel_id=1, source_target_pairs={{0,128},{4,132},{8,136},{12,140},{16,144},{20,148},{24,152},{28,15... | collective-permute-start | bytes 159752 | tf_op jit(solution)/shard_map/ppermute | solution.py:29
  102.5 6.4 %collective-permute-start.27 = (bf16[208,128]{1,0:T(8,128)(2,1)S(1)}, bf16[208,128]{1,0:T(8,128)(2,1)S(1)}, u32[]{:S(2)}, u32[]{:S(2)}) collective-permute-start(bf16[208,128]{1,0:T(8,128)(2,1)S(1)} %get-tuple-element.103), channel_id=1, source_target_pairs={{0,96},{4,100},{8,104},{12,108},{16,112},{20,116},{24,120},{28,124... | collective-permute-start | bytes 159752 | tf_op jit(solution)/shard_map/ppermute | solution.py:29
  108.8 10.3 %collective-permute-start.38 = (f32[20,640]{1,0:T(8,128)S(1)}, f32[20,640]{1,0:T(8,128)S(1)}, u32[]{:S(2)}, u32[]{:S(2)}) collective-permute-start(f32[20,640]{1,0:T(8,128)S(1)} %constant_dynamic-slice_fusion.1), channel_id=1, source_target_pairs={{0,4},{4,0},{8,12},{12,8},{16,20},{20,16},{24,28},{28,24},{32,36},... | collective-permute-start | bytes 153608 | tf_op jit(solution)/shard_map/ppermute | solution.py:29
  117.4 11.4 %collective-permute-start.37 = (bf16[8,208,128]{2,1,0:T(8,128)(2,1)S(1)}, bf16[8,208,128]{2,1,0:T(8,128)(2,1)S(1)}, u32[]{:S(2)}, u32[]{:S(2)}) collective-permute-start(bf16[8,208,128]{2,1,0:T(8,128)(2,1)S(1)} %bitcast_dynamic-update-slice_fusion.a0), channel_id=1, source_target_pairs={{0,24},{4,28},{8,0},{12,4},{16,8},{20,12},{24,16},{28,20},{32,56},... | collective-permute-start | bytes 1277960 | tf_op jit(solution)/shard_map/ppermute | solution.py:29
  118.5 12.6 %collective-permute-start.35 = (bf16[8,208,128]{2,1,0:T(8,128)(2,1)S(1)}, bf16[8,208,128]{2,1,0:T(8,128)(2,1)S(1)}, u32[]{:S(2)}, u32[]{:S(2)}) collective-permute-start(bf16[8,208,128]{2,1,0:T(8,128)(2,1)S(1)} %bitcast_dynamic-update-slice_fusion.a0), channel_id=1, source_target_pairs={{0,16},{4,20},{8,24},{12,28},{16,0},{20,4},{24,8},{28,12},{32,48},... | collective-permute-start | bytes 1277960 | tf_op jit(solution)/shard_map/ppermute | solution.py:29
  119.0 21.9 %collective-permute-start.33 = (bf16[8,208,128]{2,1,0:T(8,128)(2,1)S(1)}, bf16[8,208,128]{2,1,0:T(8,128)(2,1)S(1)}, u32[]{:S(2)}, u32[]{:S(2)}) collective-permute-start(bf16[8,208,128]{2,1,0:T(8,128)(2,1)S(1)} %bitcast_dynamic-update-slice_fusion.a0), channel_id=1, source_target_pairs={{0,8},{4,12},{8,16},{12,20},{16,24},{20,28},{24,0},{28,4},{32,40},... | collective-permute-start | bytes 1277960 | tf_op jit(solution)/shard_map/ppermute | solution.py:29
  119.9 24.2 %collective-permute-start.32 = (bf16[8,208,128]{2,1,0:T(8,128)(2,1)S(1)}, bf16[8,208,128]{2,1,0:T(8,128)(2,1)S(1)}, u32[]{:S(2)}, u32[]{:S(2)}) collective-permute-start(bf16[8,208,128]{2,1,0:T(8,128)(2,1)S(1)} %bitcast_dynamic-update-slice_fusion.a0), channel_id=1, source_target_pairs={{0,4},{4,0},{8,12},{12,8},{16,20},{20,16},{24,28},{28,24},{32,36},... | collective-permute-start | bytes 1277960 | tf_op jit(solution)/shard_map/ppermute | solution.py:29
  128.9 15.2 %collective-permute-start.39 = (bf16[8,208,128]{2,1,0:T(8,128)(2,1)S(1)}, bf16[8,208,128]{2,1,0:T(8,128)(2,1)S(1)}, u32[]{:S(2)}, u32[]{:S(2)}) collective-permute-start(bf16[8,208,128]{2,1,0:T(8,128)(2,1)S(1)} %collective-permute-done.37.a3), channel_id=1, source_target_pairs={{0,4},{4,0},{8,12},{12,8},{16,20},{20,16},{24,28},{28,24},{32,36},... | collective-permute-start | bytes 1277960 | tf_op jit(solution)/shard_map/ppermute | solution.py:29
  131.1 13.0 %collective-permute-start.36 = (bf16[8,208,128]{2,1,0:T(8,128)(2,1)S(1)}, bf16[8,208,128]{2,1,0:T(8,128)(2,1)S(1)}, u32[]{:S(2)}, u32[]{:S(2)}) collective-permute-start(bf16[8,208,128]{2,1,0:T(8,128)(2,1)S(1)} %collective-permute-done.35.a2), channel_id=1, source_target_pairs={{0,4},{4,0},{8,12},{12,8},{16,20},{20,16},{24,28},{28,24},{32,36},... | collective-permute-start | bytes 1277960 | tf_op jit(solution)/shard_map/ppermute | solution.py:29
  (14 other events, 71.3 us)
